TPU v7x, 512 devices: a whole 4x8x8 slice. The times are simulated.
512 devices in a mesh: seq: 64 (over z_lo, y, core), head: 8 (over x, z_hi).
Axes of the slice: x: 4, y: 8, z: 8 (z_hi: 2, z_lo: 4; z = z_hi * 4 + z_lo), core: 2. Of those that a mesh axis runs over, the one named last changes fastest.
Arguments:
- att_q: bfloat16 [16384, 5120], P('seq', 'head'), may hold values from -150 to 150
- att_k: bfloat16 [16384, 5120], P('seq', 'head'), may hold values from -6 to 6
- att_v: bfloat16 [16384, 5120], P('seq', 'head'), may hold values from -6 to 6
- fast_q: bfloat16 [16384, 5120], P('seq', 'head'), may hold values from -6 to 6
- fast_k: bfloat16 [16384, 5120], P('seq', 'head'), may hold values from -6 to 6
- fast_v: bfloat16 [16384, 5120], P('seq', 'head'), may hold values from -6 to 6
- learn_rates: float32 [16384], P('seq'), may hold values from 0.0002 to 0.002
- w_gate: bfloat16 [640, 5120], P(None, 'head'), may hold values from -0.25 to 0.25
- w_up: bfloat16 [640, 5120], P(None, 'head'), may hold values from -0.25 to 0.25
- w_down: bfloat16 [640, 5120], P(None, 'head'), may hold values from -0.25 to 0.25
Outputs:
- attended: bfloat16 [16384, 5120], P('seq', 'head')
- fast_out: bfloat16 [16384, 5120], P('seq', 'head')
All inputs are finite; a program needn't handle non-finite values.
Results may differ from a plain program's by a relative error of at most 0.007.
The roundings to bfloat16 on the way count: a program that leaves them out, or rounds other values in their place, can miss the bound.
Values may be sent and summed in bfloat16 or wider, within the bound.
A program may use at most 64 MiB of HBM per device.

v0:
```python
import jax
import jax.numpy as jnp
from jax import lax
from jax.sharding import Mesh
from jax.sharding import PartitionSpec as P

WINDOW = 1024
HEAD_DIM = 128
SEQ = ("seq_0", "seq_1", "seq_2")


norm_eps = 1e-06


def passed_along(value, axis, steps):
    count = lax.axis_size(axis)
    first, last = (max(0, -steps), min(count, count - steps))
    return lax.ppermute(value, axis, [(source, source + steps) for source in range(first, last)])


def filled_up(lines, peers):
    spare = -len(lines) % peers
    return jnp.pad(lines, [(0, spare)] + [(0, 0)] * (lines.ndim - 1))


def sent_to_all(value, axis):
    peers = lax.axis_size(axis)
    return lax.all_to_all(
        jnp.broadcast_to(value[None], (peers, *value.shape)), axis, 0, 0, tiled=True
    )


def in_order(blocks, dim):
    lengths = list(blocks.shape[1:])
    lengths[dim] *= blocks.shape[0]
    return jnp.moveaxis(blocks, 0, dim).reshape(lengths)


def whole_of(value, axes, dim):
    far, near = axes
    first = sent_to_all(value, far)
    blocks = jnp.swapaxes(sent_to_all(first, near), 0, 1)
    return in_order(blocks.reshape(-1, *value.shape), dim)


def split_up(value, dim, peers):
    lengths = value.shape
    blocks = value.reshape(*lengths[:dim], peers, lengths[dim] // peers, *lengths[dim + 1 :])
    return jnp.moveaxis(blocks, dim, 0)


def summed_on_arrival(value, axis, dim):
    peers = lax.axis_size(axis)
    blocks = lax.all_to_all(split_up(value, dim, peers), axis, 0, 0, tiled=True)
    return jnp.sum(blocks, axis=0)


def summed_rows(value, axes, dim):
    far, near = axes
    own = summed_on_arrival(split_up(value, dim, lax.axis_size(far)), near, dim + 1)
    return jnp.sum(lax.all_to_all(own, far, 0, 0, tiled=True), axis=0)


def nested_sum(value, axes):
    lines = value.reshape(-1, value.shape[-1])
    padded = filled_up(lines, lax.axis_size(axes[0]) * lax.axis_size(axes[1]))
    whole = whole_of(summed_rows(padded, axes, 0), axes, 0)
    return lax.slice_in_dim(whole, 0, len(lines)).reshape(value.shape)


def taken_together(value, axis):
    return sent_to_all(value, axis).sum(axis=0)


def collect(value, axis, dim):
    return in_order(sent_to_all(value, axis), dim)


def silu_slope(pre_act):
    sigmoid_v = jax.nn.sigmoid(pre_act)
    return sigmoid_v * (1.0 + pre_act * (1.0 - sigmoid_v))


def contract_rows(lhs_rows, rhs_rows):
    return lax.dot_general(
        lhs_rows, rhs_rows, (((0,), (0,)), ((), ())), preferred_element_type=jnp.float32
    )


def column_norm(old_weights):
    return jnp.sqrt(jnp.sum(old_weights * old_weights, axis=1, keepdims=True))


def full_renorm(old_weights, summed):
    updated = old_weights + summed
    col_squares = jnp.sum(updated * updated, axis=1, keepdims=True)
    return (updated * (column_norm(old_weights) / jnp.sqrt(col_squares + norm_eps))).astype(
        jnp.bfloat16
    )


def body(att_q, att_k, att_v, fast_q, fast_k, fast_v, learn_rates, w_gate, w_up, w_down):
    tok_rows = att_q.shape[0]
    head_count = att_q.shape[1] // HEAD_DIM
    hop_count = WINDOW // tok_rows
    row_start = lax.axis_index(SEQ) * tok_rows
    own_pair = jnp.stack([att_k, att_v])
    earlier = []
    moving = own_pair
    for hop_step in range(hop_count):
        moving = passed_along(moving, SEQ, 1)
        earlier.append(moving)
    key_value = jnp.concatenate(earlier[::-1] + [own_pair], axis=1)
    key_span = key_value.shape[1]
    query_block = att_q.reshape(tok_rows, head_count, HEAD_DIM)
    key_block = key_value[0].reshape(key_span, head_count, HEAD_DIM)
    val_block = key_value[1].reshape(key_span, head_count, HEAD_DIM)
    scores = jnp.einsum(
        "qhd,khd->hqk", query_block, key_block, preferred_element_type=jnp.float32
    ) * HEAD_DIM ** (-0.5)
    query_pos = row_start + jnp.arange(tok_rows, dtype=jnp.int32)
    key_pos = row_start - WINDOW + jnp.arange(key_span, dtype=jnp.int32)
    allowed = (
        (key_pos[None, :] <= query_pos[:, None])
        & (key_pos[None, :] > query_pos[:, None] - WINDOW)
        & (key_pos[None, :] >= 0)
    )
    scores = jnp.where(allowed[None], scores, jnp.float32(-1e30))
    row_max = jnp.max(scores, axis=-1, keepdims=True)
    expd = jnp.exp(scores - row_max)
    softmax_w = (expd / jnp.sum(expd, axis=-1, keepdims=True)).astype(jnp.bfloat16)
    attended = jnp.einsum("hqk,khd->qhd", softmax_w, val_block, preferred_element_type=jnp.float32)
    attended = attended.reshape(tok_rows, head_count * HEAD_DIM).astype(jnp.bfloat16)
    rate_col = learn_rates[:, None]
    pre_gate = jnp.dot(fast_k, w_gate, preferred_element_type=jnp.float32)
    pre_up = jnp.dot(fast_k, w_up, preferred_element_type=jnp.float32)
    back_proj = jnp.dot(fast_v, w_down, preferred_element_type=jnp.float32)
    gate_term = (rate_col * back_proj * pre_up * silu_slope(pre_gate)).astype(jnp.bfloat16)
    up_term = (rate_col * back_proj * jax.nn.silu(pre_gate)).astype(jnp.bfloat16)
    down_term = (rate_col * jax.nn.silu(pre_gate) * pre_up).astype(jnp.bfloat16)
    pair_grads = jnp.stack([contract_rows(fast_k, gate_term), contract_rows(fast_k, up_term)])
    down_grads = contract_rows(fast_v, down_term)[None]
    old_pair = jnp.stack([w_gate, w_up]).astype(jnp.float32)
    old_down = w_down.astype(jnp.float32)[None]
    shard_len = old_pair.shape[1] // lax.axis_size(SEQ)
    shard_start = lax.axis_index(SEQ) * shard_len
    fresh_pair = full_renorm(old_pair, nested_sum(pair_grads, (("seq_0", "seq_1"), "seq_2")))
    summed = summed_rows(down_grads, (("seq_0", "seq_1"), "seq_2"), 1)
    updated = lax.dynamic_slice_in_dim(old_down, shard_start, shard_len, 1) + summed
    col_squares = taken_together(jnp.sum(updated * updated, axis=1, keepdims=True), SEQ)
    scaled = (updated * (column_norm(old_down) / jnp.sqrt(col_squares + norm_eps))).astype(
        jnp.bfloat16
    )
    fresh_down = collect(scaled, SEQ, 1)
    gate_q = jnp.dot(fast_q, fresh_pair[0], preferred_element_type=jnp.float32)
    up_q = jnp.dot(fast_q, fresh_pair[1], preferred_element_type=jnp.float32)
    hidden_q = (jax.nn.silu(gate_q) * up_q).astype(jnp.bfloat16)
    fast_out = jnp.einsum(
        "th,dh->td", hidden_q, fresh_down[0], preferred_element_type=jnp.float32
    ).astype(jnp.bfloat16)
    return (attended, fast_out)


def solution(mesh):
    finer = Mesh(
        mesh.devices.reshape(4, 8, 2, mesh.shape["head"]), ("seq_0", "seq_1", "seq_2", "head")
    )
    return jax.shard_map(
        body,
        mesh=finer,
        in_specs=(
            P(SEQ, "head"),
            P(SEQ, "head"),
            P(SEQ, "head"),
            P(SEQ, "head"),
            P(SEQ, "head"),
            P(SEQ, "head"),
            P(SEQ),
            P(None, "head"),
            P(None, "head"),
            P(None, "head"),
        ),
        out_specs=(P(SEQ, "head"), P(SEQ, "head")),
        check_vma=False,
    )
```

profile of v0, /device:TPU:475, one launch (start us, length us, event | category | flops | bytes accessed | tf_op | source)
XLA Modules:
  0.0 311.0 jit_solution(6685097800895732492)
XLA Ops:
  0.7 0.9 copy-done
  1.6 1.6 fusion.36
  3.2 1.8 fusion.35
  5.1 0.8 copy-done.9
  5.9 1.8 convolution_bitcast_fusion
  7.7 1.5 reshape_transpose_reshape_broadcast_in_dim.3
  9.2 1.0 copy.106
  10.2 5.4 %all_to_all.40 = f32[2,32,1,10,640]{4,1,3,2,0:T(8,128)S(1)} all-to-all(f32[2,32,1,10,640]{4,1,3,2,0:T(8,128)S(1)} %copy.106), channel_id=1, replica_groups=mesh['seq_0'=4,'seq_1'=8,'seq_2'=2,'head'=8] {'seq_2'}, dimensions={0} | all-to-all | bytes 3276800 | tf_op jit(solution)/shard_map/all_to_all | solution.py:54
  15.6 1.1 reduce_sum.106
  16.6 3.0 copy.107
  19.6 9.8 %all-to-all-start.5 = ((f32[32,1,10,640]{3,1,2,0:T(1,128)}), f32[32,1,10,640]{3,1,2,0:T(1,128)S(1)}, u32[]{:S(2)}, u32[]{:S(2)}) async-start(f32[32,1,10,640]{3,1,2,0:T(1,128)} %copy.107), calls=%async_computation.5 | async-start | bytes 1638400 | tf_op jit(solution)/shard_map/all_to_all | solution.py:61
  29.4 1.4 convert_element_type.57
  30.8 0.5 convolution_multiply_fusion
  31.3 0.5 convolution_bitcast_fusion.1
  31.9 0.6 convolution_bitcast_fusion.2
  32.5 1.9 pad_maximum_fusion
  34.4 4.6 %reshape_reshape.3 = f32[32,2,20,640]{3,2,1,0:T(8,128)} reshape(f32[2,640,640]{2,1,0:T(8,128)} %pad_maximum_fusion) | data formatting | bytes 6553600 | tf_op jit(solution)/shard_map/reshape;reshape | solution.py:48
  39.0 4.9 %copy.100 = f32[2,32,20,640]{3,1,2,0:T(8,128)} copy(f32[2,32,20,640]{3,2,0,1:T(8,128)} %bitcast.75) | data formatting | bytes 6553600 | tf_op jit(solution)/shard_map/transpose | solution.py:49
  43.9 5.3 %all-to-all-done.5 = f32[32,1,10,640]{3,1,2,0:T(1,128)S(1)} async-done(((f32[32,1,10,640]{3,1,2,0:T(1,128)}), f32[32,1,10,640]{3,1,2,0:T(1,128)S(1)}, u32[]{:S(2)}, u32[]{:S(2)}) %all-to-all-start.5) | async-done | bytes 819232 | tf_op jit(solution)/shard_map/all_to_all | solution.py:61
  49.3 7.1 %all-to-all-start = ((f32[2,32,20,640]{3,1,2,0:T(8,128)}), f32[2,32,20,640]{3,1,2,0:T(8,128)}, u32[]{:S(2)}, u32[]{:S(2)}) async-start(f32[2,32,20,640]{3,1,2,0:T(8,128)} %copy.100), calls=%async_computation | async-start | bytes 6553600 | tf_op jit(solution)/shard_map/all_to_all | solution.py:54
  56.4 0.5 reduce_sum.108
  56.9 0.9 multiply_reduce_fusion.3
  57.7 2.1 all-to-all-done
  59.9 0.8 broadcast_in_dim.24
  60.6 8.6 %all-to-all-start.6 = ((f32[64,1,1,640]{3,2,1,0:T(1,128)}), f32[64,1,1,640]{3,2,1,0:T(1,128)S(1)}, u32[]{:S(2)}, u32[]{:S(2)}) async-start(f32[64,1,1,640]{3,2,1,0:T(1,128)} %broadcast_in_dim.24), calls=%async_computation.6 | async-start | bytes 327680 | tf_op jit(solution)/shard_map/all_to_all | solution.py:28
  69.2 2.3 reduce_sum.100
  71.5 2.2 copy.101
  73.8 2.2 all-to-all-done.6
  75.9 0.7 copy-done.11
  76.6 7.7 %all-to-all-start.1 = ((f32[32,20,640]{2,1,0:T(8,128)}), f32[32,20,640]{2,1,0:T(8,128)S(1)}, u32[]{:S(2)}, u32[]{:S(2)}) async-start(f32[32,20,640]{2,1,0:T(8,128)} %copy.101), calls=%async_computation.1 | async-start | bytes 3932160 | tf_op jit(solution)/shard_map/all_to_all | solution.py:61
  84.5 1.1 copy.95
  85.8 1.0 reduce_sum.111
  86.9 0.9 multiply_convert_fusion.7
  87.7 44.3 %all-to-all-done.1 = f32[32,20,640]{2,1,0:T(8,128)S(1)} async-done(((f32[32,20,640]{2,1,0:T(8,128)}), f32[32,20,640]{2,1,0:T(8,128)S(1)}, u32[]{:S(2)}, u32[]{:S(2)}) %all-to-all-start.1) | async-done | bytes 1638432 | tf_op jit(solution)/shard_map/all_to_all | solution.py:61
  132.1 1.2 broadcast_in_dim.25
  133.2 11.1 %all-to-all-start.7 = ((bf16[64,1,10,640]{3,2,1,0:T(8,128)(2,1)}), bf16[64,1,10,640]{3,2,1,0:T(8,128)(2,1)}, u32[]{:S(2)}, u32[]{:S(2)}) async-start(bf16[64,1,10,640]{3,2,1,0:T(8,128)(2,1)} %broadcast_in_dim.25), calls=%async_computation.7 | async-start | bytes 2621440 | tf_op jit(solution)/shard_map/all_to_all | solution.py:28
  144.4 4.6 %collective-permute-start = (bf16[2,256,640]{1,2,0:T(8,128)(2,1)S(1)}, bf16[2,256,640]{1,2,0:T(8,128)(2,1)S(1)}, u32[]{:S(2)}, u32[]{:S(2)}) collective-permute-start(bf16[2,256,640]{1,2,0:T(8,128)(2,1)S(1)} %pad_maximum_fusion.1), channel_id=1, source_target_pairs={{0,8},{8,16},{16,24},{24,32},{32,40},{40,48},{48,56},{56,64},{64,7... | collective-permute-start | bytes 1966088 | tf_op jit(solution)/shard_map/ppermute | solution.py:18
  149.0 30.6 %collective-permute-done = bf16[2,256,640]{1,2,0:T(8,128)(2,1)S(1)} collective-permute-done((bf16[2,256,640]{1,2,0:T(8,128)(2,1)S(1)}, bf16[2,256,640]{1,2,0:T(8,128)(2,1)S(1)}, u32[]{:S(2)}, u32[]{:S(2)}) %collective-permute-start) | collective-permute-done | bytes 655392 | tf_op jit(solution)/shard_map/ppermute | solution.py:18
  179.6 5.6 %collective-permute-start.1 = (bf16[2,256,640]{1,2,0:T(8,128)(2,1)S(1)}, bf16[2,256,640]{1,2,0:T(8,128)(2,1)}, u32[]{:S(2)}, u32[]{:S(2)}) collective-permute-start(bf16[2,256,640]{1,2,0:T(8,128)(2,1)S(1)} %collective-permute-done), channel_id=1, source_target_pairs={{0,8},{8,16},{16,24},{24,32},{32,40},{40,48},{48,56},{56,64},{64,7... | collective-permute-start | bytes 1966088 | tf_op jit(solution)/shard_map/ppermute | solution.py:18
  185.2 7.5 %collective-permute-done.1 = bf16[2,256,640]{1,2,0:T(8,128)(2,1)} collective-permute-done((bf16[2,256,640]{1,2,0:T(8,128)(2,1)S(1)}, bf16[2,256,640]{1,2,0:T(8,128)(2,1)}, u32[]{:S(2)}, u32[]{:S(2)}) %collective-permute-start.1) | collective-permute-done | bytes 655392 | tf_op jit(solution)/shard_map/ppermute | solution.py:18
  192.7 5.7 %collective-permute-start.2 = (bf16[2,256,640]{1,2,0:T(8,128)(2,1)}, bf16[2,256,640]{1,2,0:T(8,128)(2,1)}, u32[]{:S(2)}, u32[]{:S(2)}) collective-permute-start(bf16[2,256,640]{1,2,0:T(8,128)(2,1)} %collective-permute-done.1), channel_id=1, source_target_pairs={{0,8},{8,16},{16,24},{24,32},{32,40},{40,48},{48,56},{56,64},{64,7... | collective-permute-start | bytes 1966088 | tf_op jit(solution)/shard_map/ppermute | solution.py:18
  198.6 1.4 broadcast_in_dim.22
  200.0 7.8 %all-to-all-start.2 = ((f32[32,20,640]{2,1,0:T(8,128)}), f32[32,20,640]{2,1,0:T(8,128)}, u32[]{:S(2)}, u32[]{:S(2)}) async-start(f32[32,20,640]{2,1,0:T(8,128)} %broadcast_in_dim.22), calls=%async_computation.2 | async-start | bytes 3932160 | tf_op jit(solution)/shard_map/all_to_all | solution.py:28
  207.8 0.9 copy.96
  208.7 1.9 maximum_convert_fusion
  210.7 4.6 %reshape.156 = f32[32,2,20,640]{3,2,1,0:T(8,128)} reshape(f32[2,640,640]{2,1,0:T(8,128)} %maximum_convert_fusion) | data formatting | bytes 6553600 | tf_op jit(solution)/shard_map/convert_element_type | solution.py:143
  215.3 4.3 %collective-permute-start.3 = (bf16[2,256,640]{1,2,0:T(8,128)(2,1)}, bf16[2,256,640]{1,2,0:T(8,128)(2,1)S(1)}, u32[]{:S(2)}, u32[]{:S(2)}) collective-permute-start(bf16[2,256,640]{1,2,0:T(8,128)(2,1)} %collective-permute-done.2), channel_id=1, source_target_pairs={{0,8},{8,16},{16,24},{24,32},{32,40},{40,48},{48,56},{56,64},{64,7... | collective-permute-start | bytes 1966088 | tf_op jit(solution)/shard_map/ppermute | solution.py:18
  220.0 1.0 and_and_fusion
  220.9 40.3 %collective-permute-done.3 = bf16[2,256,640]{1,2,0:T(8,128)(2,1)S(1)} collective-permute-done((bf16[2,256,640]{1,2,0:T(8,128)(2,1)}, bf16[2,256,640]{1,2,0:T(8,128)(2,1)S(1)}, u32[]{:S(2)}, u32[]{:S(2)}) %collective-permute-start.3) | collective-permute-done | bytes 655392 | tf_op jit(solution)/shard_map/ppermute | solution.py:18
  261.2 1.1 constant_dynamic-update-slice_fusion.3
  262.4 1.1 constant_dynamic-update-slice_fusion.2
  263.6 1.9 fusion.33
  265.6 3.9 %fusion.34 = f32[5,256]{1,0:T(8,128)S(1)} fusion(pred[256,1280]{0,1:T(8,128)(4,1)S(1)} %and_and_fusion, bf16[1280,5,128]{0,2,1:T(8,128)(2,1)} %bitcast.89, bf16[256,5,128]{0,2,1:T(8,128)(2,1)S(1)} %bitcast.92), kind=kOutput, calls=%fused_computation.69 | convolution fusion | flops 425985280 | bytes 2298880 | tf_op jit(solution)/shard_map/sub | solution.py:130
  269.5 5.0 %fusion.8 = bf16[5,128,256]{2,1,0:T(8,128)(2,1)S(1)} fusion(bf16[1280,5,128]{0,2,1:T(8,128)(2,1)} %bitcast.91, f32[5,256]{1,0:T(8,128)S(1)} %fusion.34, pred[256,1280]{0,1:T(8,128)(4,1)S(1)} %and_and_fusion, bf16[1280,5,128]{0,2,1:T(8,128)(2,1)} %bitcast.90, bf16[256,5,128]{0,2,1:T(8,128)(2,1)S(1)} %bitcast.93), kind=kOutput, calls=%fused_computation.26 | convolution fusion | flops 847219200 | bytes 4264960 | tf_op jit(solution)/shard_map/hqk,khd->qhd/dot_general | solution.py:132
  274.6 0.9 copy.109
  275.5 1.4 squeeze_reshape_transpose.3
  276.9 1.9 copy.102
  279.2 14.4 %all_to_all.41 = f32[2,32,20,640]{3,1,2,0:T(8,128)S(1)} all-to-all(f32[2,32,20,640]{3,1,2,0:T(8,128)S(1)} %broadcast_in_dim.23), channel_id=1, replica_groups=mesh['seq_0'=4,'seq_1'=8,'seq_2'=2,'head'=8] {'seq_2'}, dimensions={0} | all-to-all | bytes 6553600 | tf_op jit(solution)/shard_map/all_to_all | solution.py:28
  293.6 2.1 multiply_reduce_fusion
  295.8 3.8 %copy.119 = f32[2,32,20,640]{3,2,0,1:T(8,128)} copy(f32[2,32,20,640]{3,1,2,0:T(8,128)S(1)} %all_to_all.41) | data formatting | bytes 6553600 | tf_op jit(solution)/shard_map/all_to_all | solution.py:28
  299.6 4.7 %reshape_reshape_reshape.3 = f32[2,640,640]{2,1,0:T(8,128)} reshape(f32[32,2,20,640]{3,2,1,0:T(8,128)} %bitcast.76) | data formatting | bytes 6553600 | tf_op jit(solution)/shard_map/reshape;reshape;reshape | solution.py:68
  304.3 2.4 multiply_convert_fusion
  306.7 1.2 copy-done.6
  308.3 2.7 convolution_convert_fusion
  (51 shorter events, 2.2 us)
Async XLA Ops:
  0.6 1.0 copy-start
  0.6 5.3 %copy-start.16 = (bf16[256,640]{1,0:T(8,128)(2,1)S(1)}, bf16[256,640]{1,0:T(8,128)(2,1)}, u32[]{:S(2)}) copy-start(bf16[256,640]{1,0:T(8,128)(2,1)} %param.15) | copy-start | bytes 983044
  0.7 5.3 %copy-start.17 = (f32[256]{0:T(256)S(1)}, f32[256]{0:T(256)}, u32[]{:S(2)}) copy-start(f32[256]{0:T(256)} %param.16) | copy-start | bytes 3076
  3.2 1.9 copy-start.7
  5.1 0.8 copy-start.9
  15.6 13.9 %copy-start.5 = (bf16[640,640]{1,0:T(8,128)(2,1)S(1)}, bf16[640,640]{1,0:T(8,128)(2,1)}, u32[]{:S(2)}) copy-start(bf16[640,640]{1,0:T(8,128)(2,1)} %param.19) | copy-start | bytes 2457604
  19.6 11.7 %copy-start.8 = (f32[256,640]{1,0:T(8,128)S(1)}, f32[256,640]{1,0:T(8,128)}, u32[]{:S(2)}) copy-start(f32[256,640]{1,0:T(8,128)} %copy-done.7) | copy-start | bytes 1966084
  19.6 29.7 %all-to-all-start.5 = ((f32[32,1,10,640]{3,1,2,0:T(1,128)}), f32[32,1,10,640]{3,1,2,0:T(1,128)S(1)}, u32[]{:S(2)}, u32[]{:S(2)}) async-start(f32[32,1,10,640]{3,1,2,0:T(1,128)} %copy.107), calls=%async_computation.5 | async-start | bytes 1638400 | tf_op jit(solution)/shard_map/all_to_all | solution.py:61
  30.8 1.1 copy-start.10
  49.3 10.6 %all-to-all-start = ((f32[2,32,20,640]{3,1,2,0:T(8,128)}), f32[2,32,20,640]{3,1,2,0:T(8,128)}, u32[]{:S(2)}, u32[]{:S(2)}) async-start(f32[2,32,20,640]{3,1,2,0:T(8,128)} %copy.100), calls=%async_computation | async-start | bytes 6553600 | tf_op jit(solution)/shard_map/all_to_all | solution.py:54
  60.6 15.3 %all-to-all-start.6 = ((f32[64,1,1,640]{3,2,1,0:T(1,128)}), f32[64,1,1,640]{3,2,1,0:T(1,128)S(1)}, u32[]{:S(2)}, u32[]{:S(2)}) async-start(f32[64,1,1,640]{3,2,1,0:T(1,128)} %broadcast_in_dim.24), calls=%async_computation.6 | async-start | bytes 327680 | tf_op jit(solution)/shard_map/all_to_all | solution.py:28
  71.5 12.8 %copy-start.13 = (bf16[256,640]{1,0:T(8,128)(2,1)S(1)}, bf16[256,640]{1,0:T(8,128)(2,1)}, u32[]{:S(2)}) copy-start(bf16[256,640]{1,0:T(8,128)(2,1)} %param.11) | copy-start | bytes 983044
  75.9 0.7 copy-start.11
  76.6 55.5 %all-to-all-start.1 = ((f32[32,20,640]{2,1,0:T(8,128)}), f32[32,20,640]{2,1,0:T(8,128)S(1)}, u32[]{:S(2)}, u32[]{:S(2)}) async-start(f32[32,20,640]{2,1,0:T(8,128)} %copy.101), calls=%async_computation.1 | async-start | bytes 3932160 | tf_op jit(solution)/shard_map/all_to_all | solution.py:61
  133.2 65.3 %all-to-all-start.7 = ((bf16[64,1,10,640]{3,2,1,0:T(8,128)(2,1)}), bf16[64,1,10,640]{3,2,1,0:T(8,128)(2,1)}, u32[]{:S(2)}, u32[]{:S(2)}) async-start(bf16[64,1,10,640]{3,2,1,0:T(8,128)(2,1)} %broadcast_in_dim.25), calls=%async_computation.7 | async-start | bytes 2621440 | tf_op jit(solution)/shard_map/all_to_all | solution.py:28
  144.4 35.2 %collective-permute-start = (bf16[2,256,640]{1,2,0:T(8,128)(2,1)S(1)}, bf16[2,256,640]{1,2,0:T(8,128)(2,1)S(1)}, u32[]{:S(2)}, u32[]{:S(2)}) collective-permute-start(bf16[2,256,640]{1,2,0:T(8,128)(2,1)S(1)} %pad_maximum_fusion.1), channel_id=1, source_target_pairs={{0,8},{8,16},{16,24},{24,32},{32,40},{40,48},{48,56},{56,64},{64,7... | collective-permute-start | bytes 1966088 | tf_op jit(solution)/shard_map/ppermute | solution.py:18
  179.6 13.1 %collective-permute-start.1 = (bf16[2,256,640]{1,2,0:T(8,128)(2,1)S(1)}, bf16[2,256,640]{1,2,0:T(8,128)(2,1)}, u32[]{:S(2)}, u32[]{:S(2)}) collective-permute-start(bf16[2,256,640]{1,2,0:T(8,128)(2,1)S(1)} %collective-permute-done), channel_id=1, source_target_pairs={{0,8},{8,16},{16,24},{24,32},{32,40},{40,48},{48,56},{56,64},{64,7... | collective-permute-start | bytes 1966088 | tf_op jit(solution)/shard_map/ppermute | solution.py:18
  192.7 22.6 %collective-permute-start.2 = (bf16[2,256,640]{1,2,0:T(8,128)(2,1)}, bf16[2,256,640]{1,2,0:T(8,128)(2,1)}, u32[]{:S(2)}, u32[]{:S(2)}) collective-permute-start(bf16[2,256,640]{1,2,0:T(8,128)(2,1)} %collective-permute-done.1), channel_id=1, source_target_pairs={{0,8},{8,16},{16,24},{24,32},{32,40},{40,48},{48,56},{56,64},{64,7... | collective-permute-start | bytes 1966088 | tf_op jit(solution)/shard_map/ppermute | solution.py:18
  198.5 9.3 %copy-start.14 = (bf16[256,640]{1,0:T(8,128)(2,1)S(1)}, bf16[256,640]{1,0:T(8,128)(2,1)}, u32[]{:S(2)}) copy-start(bf16[256,640]{1,0:T(8,128)(2,1)} %param.10) | copy-start | bytes 983044
  198.5 10.2 %copy-start.3 = (bf16[640,640]{1,0:T(8,128)(2,1)S(1)}, bf16[640,640]{1,0:T(8,128)(2,1)}, u32[]{:S(2)}) copy-start(bf16[640,640]{1,0:T(8,128)(2,1)} %param.18) | copy-start | bytes 2457604
  198.5 10.2 %copy-start.4 = (bf16[640,640]{1,0:T(8,128)(2,1)S(1)}, bf16[640,640]{1,0:T(8,128)(2,1)}, u32[]{:S(2)}) copy-start(bf16[640,640]{1,0:T(8,128)(2,1)} %param.17) | copy-start | bytes 2457604
  200.0 76.9 %all-to-all-start.2 = ((f32[32,20,640]{2,1,0:T(8,128)}), f32[32,20,640]{2,1,0:T(8,128)}, u32[]{:S(2)}, u32[]{:S(2)}) async-start(f32[32,20,640]{2,1,0:T(8,128)} %broadcast_in_dim.22), calls=%async_computation.2 | async-start | bytes 3932160 | tf_op jit(solution)/shard_map/all_to_all | solution.py:28
  215.3 45.9 %collective-permute-start.3 = (bf16[2,256,640]{1,2,0:T(8,128)(2,1)}, bf16[2,256,640]{1,2,0:T(8,128)(2,1)S(1)}, u32[]{:S(2)}, u32[]{:S(2)}) collective-permute-start(bf16[2,256,640]{1,2,0:T(8,128)(2,1)} %collective-permute-done.2), channel_id=1, source_target_pairs={{0,8},{8,16},{16,24},{24,32},{32,40},{40,48},{48,56},{56,64},{64,7... | collective-permute-start | bytes 1966088 | tf_op jit(solution)/shard_map/ppermute | solution.py:18
  263.6 1.9 copy-start.15
  279.2 14.4 %copy-start.2 = (f32[32,2,20,640]{3,2,1,0:T(8,128)S(1)}, f32[32,2,20,640]{3,2,1,0:T(8,128)}, u32[]{:S(2)}) copy-start(f32[32,2,20,640]{3,2,1,0:T(8,128)} %reshape.156) | copy-start | bytes 9830404
  304.3 3.6 %copy-start.12 = (bf16[256,640]{1,0:T(8,128)(2,1)S(1)}, bf16[256,640]{1,0:T(8,128)(2,1)}, u32[]{:S(2)}) copy-start(bf16[256,640]{1,0:T(8,128)(2,1)} %param.13) | copy-start | bytes 983044
  306.7 1.2 copy-start.6
  307.9 3.1 %copy-start.1 = (bf16[256,640]{1,0:T(8,128)(2,1)S(1)}, bf16[256,640]{1,0:T(8,128)(2,1)}, u32[]{:S(2)}) copy-start(bf16[256,640]{1,0:T(8,128)(2,1)} %param.14) | copy-start | bytes 983044
where the time goes:
time: 313 us; the launch traced here: 311 us
  waiting for transfers between devices  132 us (42%)
  starting transfers between devices  72.3 us (23%)
  local copies, waits for them, and re-layouts  48.6 us (16%)
  blocking collectives  19.7 us (6%)
  matrix products  18.9 us (6%)
  other arithmetic  18.1 us (6%)
    ppermute x4, waiting for transfers between devices, passed_along(): lax.ppermute(value, axis, [(source, source + steps) for source in range(f...  78.4 us
    all_to_all x2, waiting for transfers between devices, summed_rows(): return jnp.sum(lax.all_to_all(own, far, 0, 0, tiled=True), axis=0)  49.7 us
    all_to_all x3, starting transfers between devices, sent_to_all(): lax.all_to_all(jnp.broadcast_to(value[None], (peers, *value.shape)), axis...  27.5 us
    ppermute x4, starting transfers between devices, passed_along(): lax.ppermute(value, axis, [(source, source + steps) for source in range(f...  20.2 us
    all_to_all x2, starting transfers between devices, summed_rows(): return jnp.sum(lax.all_to_all(own, far, 0, 0, tiled=True), axis=0)  17.5 us
    all_to_all x1, blocking collectives, sent_to_all(): lax.all_to_all(jnp.broadcast_to(value[None], (peers, *value.shape)), axis...  14.4 us
    unnamed x44, local copies, waits for them, and re-layouts  9.27 us
    all_to_all x1, starting transfers between devices, summed_on_arrival(): blocks = lax.all_to_all(split_up(value, dim, peers), axis, 0, 0, tiled=True)  7.12 us
  transfers between devices with their start and end apart: 10, of which 7 were waited for; matrix products, arithmetic and copies ran while one was open for 16% of the time, Pallas kernels for 0%

commit v1 on v0

v1 whole, which is shorter than its diff:
```python
import functools

import jax
import jax.numpy as jnp
from jax import lax
from jax.experimental import pallas as pl
from jax.experimental.pallas import tpu as pltpu
from jax.sharding import PartitionSpec as P

HEAD_DIM = 128
BLK = 128
HOPS = 4
NORM_EPS = 1e-06
MASKED = -1e30
MESH = pl.DeviceIdType.MESH
F32 = jnp.float32
BF16 = jnp.bfloat16


def silu_parts(pre_act):
    sig = jax.nn.sigmoid(pre_act)
    return pre_act * sig, sig * (1.0 + pre_act * (1.0 - sig))


def contract_rows(lhs, rhs):
    return lax.dot_general(lhs, rhs, (((0,), (0,)), ((), ())), preferred_element_type=F32)


def contract_cols(lhs, rhs):
    return lax.dot_general(lhs, rhs, (((1,), (1,)), ((), ())), preferred_element_type=F32)


def kernel(
    ny, nz,
    aq_h, ak_h, av_h, fq_h, fk_h, fv_h, lr_h, wg_h, wu_h, wd_h,
    att_h, out_h,
    aq, okv, halo, fq, kvf, lr, w3, tt, rt, grad, ry, zs, zr, old_t, fresh,
    m_s, l_s, acc_s, att_v, out_v,
    loc, osem, hs, hr, ps, pr, ts, tr, rs_s, rs_r, zs_s, zs_r, az_s, az_r, ag_s, ag_r, ad_s, ad_r,
):
    tok, feat = aq.shape
    nb = w3.shape[2] // BLK
    heads = feat // HEAD_DIM
    half = BLK // 2
    zrow = BLK // nz
    s = lax.axis_index("seq")
    total = 2 * ny * nz
    c = lax.rem(s, 2)
    y = lax.rem(s // 2, ny)
    z = s // (2 * ny)
    mate = s + 1 - 2 * c
    y_next = z * 2 * ny + lax.rem(y + 1, ny) * 2 + c
    y_prev = z * 2 * ny + lax.rem(y + ny - 1, ny) * 2 + c
    z_peer = [lax.rem(z + i, nz) * 2 * ny + y * 2 + c for i in range(1, nz)]
    chain = {(0, 0): ny // 2, (0, 1): ny // 2 - 1, (1, 0): ny // 2 - 1, (1, 1): ny // 2}
    max_hop = ny // 2

    def remote(src, dst, ssem, rsem, dev):
        return pltpu.make_async_remote_copy(
            src_ref=src, dst_ref=dst, send_sem=ssem, recv_sem=rsem,
            device_id={"seq": dev}, device_id_type=MESH,
        )

    loads = [
        (fk_h, kvf.at[0, 0]), (wg_h, w3.at[0]), (wu_h, w3.at[1]), (lr_h, lr),
        (fv_h, kvf.at[0, 1]), (wd_h, w3.at[2]),
        (aq_h, aq), (ak_h, okv.at[0]), (av_h, okv.at[1]), (fq_h, fq),
    ]
    loads = [pltpu.make_async_copy(src, dst, loc.at[i]) for i, (src, dst) in enumerate(loads)]
    for one in loads:
        one.start()

    barrier = pltpu.get_barrier_semaphore()
    for peer in [mate, y_next, y_prev] + z_peer:
        pl.semaphore_signal(barrier, inc=1, device_id={"seq": peer}, device_id_type=MESH)

    @pl.when((c == 1) & (s < total - 1))
    def _():
        pl.semaphore_signal(barrier, inc=1, device_id={"seq": s + 1}, device_id_type=MESH)

    @pl.when((c == 0) & (s > 0))
    def _():
        pl.semaphore_signal(barrier, inc=1, device_id={"seq": s - 1}, device_id_type=MESH)

    beside = c * (1 - s // (total - 1)) + (1 - c) * ((s + total - 1) // total)
    pl.semaphore_wait(barrier, 3 + len(z_peer) + beside)

    def halo_copy(step, part, dev):
        if step == 0:
            src = (ak_h, av_h)[part]
        else:
            src = halo.at[step - 1, part]
        return remote(src, halo.at[step, part], hs.at[step, part], hr.at[step, part], dev)

    def halo_send(step):
        @pl.when((s < total - 1) & (s >= step))
        def _():
            for part in range(2):
                halo_copy(step, part, s + 1).start()

    def halo_send_wait(step):
        @pl.when((s < total - 1) & (s >= step))
        def _():
            for part in range(2):
                halo_copy(step, part, s + 1).wait_send()

    def halo_wait(step):
        @pl.when(s >= step + 1)
        def _():
            for part in range(2):
                halo_copy(step, part, s - 1).wait_recv()

    def pair_copy(part):
        return remote((fk_h, fv_h)[part], kvf.at[1, part], ps.at[part], pr.at[part], mate)

    for part in range(2):
        pair_copy(part).start()
    halo_send(0)

    scale = HEAD_DIM ** (-0.5)

    def attend(delta, lo, hi):
        def one_head(h, _):
            cols = pl.ds(pl.multiple_of(h * HEAD_DIM, HEAD_DIM), HEAD_DIM)
            kv = okv if delta == 0 else halo.at[delta - 1]
            key, val = kv[0, :, cols], kv[1, :, cols]
            sc = contract_cols(aq[:, cols], key) * scale
            if delta in (0, HOPS):
                qi = lax.broadcasted_iota(jnp.int32, (tok, tok), 0)
                ki = lax.broadcasted_iota(jnp.int32, (tok, tok), 1)
                keep = (ki <= qi) if delta == 0 else (ki > qi)
                sc = jnp.where(keep, sc, MASKED)
            top = jnp.max(sc, axis=1, keepdims=True)
            if delta == 0:
                p = jnp.exp(sc - top)
                m_s[h] = top
                l_s[h] = jnp.sum(p, axis=1, keepdims=True)
                acc_s[h] = jnp.dot(p.astype(BF16), val, preferred_element_type=F32)
            else:
                m_old = m_s[h]
                m_new = jnp.maximum(m_old, top)
                p = jnp.exp(sc - m_new)
                alpha = jnp.exp(m_old - m_new)
                m_s[h] = m_new
                l_s[h] = l_s[h] * alpha + jnp.sum(p, axis=1, keepdims=True)
                acc_s[h] = acc_s[h] * alpha + jnp.dot(p.astype(BF16), val, preferred_element_type=F32)
            return 0

        if delta == 0:
            lax.fori_loop(lo, hi, one_head, 0)
        else:
            @pl.when(s >= delta)
            def _():
                lax.fori_loop(lo, hi, one_head, 0)

    loads[0].wait()
    loads[1].wait()
    loads[2].wait()
    loads[3].wait()
    keys = kvf[0, 0]
    eye = lax.broadcasted_iota(jnp.int32, (tok, tok), 0) == lax.broadcasted_iota(jnp.int32, (tok, tok), 1)
    rate = jnp.sum(jnp.where(eye, jnp.broadcast_to(lr[...], (tok, tok)), 0.0), axis=1, keepdims=True)
    if 2 * ny > 3 * nb:
        for b in range(3 * nb, 2 * ny):
            tt[b % 2, :, (b // 2) * BLK:(b // 2 + 1) * BLK] = jnp.zeros((tok, BLK), BF16)

    def put(b, value):
        tt[b % 2, :, (b // 2) * BLK:(b // 2 + 1) * BLK] = value.astype(BF16)

    pre_gate = jnp.dot(keys, w3[0], preferred_element_type=F32)
    pre_up = jnp.dot(keys, w3[1], preferred_element_type=F32)
    loads[4].wait()
    loads[5].wait()
    back = jnp.dot(kvf[0, 1], w3[2], preferred_element_type=F32)
    for i in range(nb):
        cols = slice(i * BLK, (i + 1) * BLK)
        pg, pu, bk = pre_gate[:, cols], pre_up[:, cols], back[:, cols]
        silu, slope = silu_parts(pg)
        rb = rate * bk
        put(i, rb * pu * slope)
        put(nb + i, rb * silu)
        put(2 * nb + i, rate * silu * pu)
    term_copy = remote(tt.at[1 - c], rt, ts, tr, mate)
    term_copy.start()

    split = nb * BLK
    width = ny * BLK
    grad[0:nb] = contract_rows(tt[c, :, 0:split], kvf[0, 0]).reshape(nb, BLK, feat)
    grad[nb:ny] = contract_rows(tt[c, :, split:width], kvf[0, 1]).reshape(ny - nb, BLK, feat)
    for i in range(6, 9):
        loads[i].wait()
    attend(0, 0, heads // 2)
    term_copy.wait_recv()
    for part in range(2):
        pair_copy(part).wait_recv()
    grad[0:nb] += contract_rows(rt[:, 0:split], kvf[1, 0]).reshape(nb, BLK, feat)
    grad[nb:ny] += contract_rows(rt[:, split:width], kvf[1, 1]).reshape(ny - nb, BLK, feat)

    rows_of = [pl.ds(0, half), pl.ds(half, half)]
    slot = {}
    for way in range(2):
        for part in range(2):
            for hop in range(chain[way, part]):
                slot[way, part, hop] = len(slot)

    def toward(way, dist):
        return lax.rem(y + dist, ny) if way == 0 else lax.rem(y + ny - dist, ny)

    def rs_copy(way, part, hop):
        if hop == 0:
            src = grad.at[toward(way, chain[way, part]), rows_of[part]]
        else:
            src = ry.at[slot[way, part, hop - 1]]
        n = slot[way, part, hop]
        return remote(src, ry.at[n], rs_s.at[n], rs_r.at[n], (y_next, y_prev)[way])

    order = [(0, 0), (1, 1), (0, 1), (1, 0)]
    for way, part in order:
        if chain[way, part] > 0:
            rs_copy(way, part, 0).start()
    attend(0, heads // 2, heads)
    for hop in range(max_hop):
        for way, part in order:
            if hop >= chain[way, part]:
                continue
            rs_copy(way, part, hop).wait_recv()
            if hop + 1 < chain[way, part]:
                n = slot[way, part, hop]
                ry[n] += grad[toward(way, chain[way, part] - hop - 1), rows_of[part]]
                rs_copy(way, part, hop + 1).start()
        if hop < HOPS - 1:
            halo_wait(hop)
            halo_send(hop + 1)
            attend(hop + 1, 0, heads)
    for part in range(2):
        got = grad[y, rows_of[part]]
        for way in range(2):
            if chain[way, part] > 0:
                got += ry[slot[way, part, chain[way, part] - 1]]
        zs[rows_of[part]] = got

    def z_rows(i):
        return pl.ds(pl.multiple_of(lax.rem(z + i, nz) * zrow, zrow), zrow)

    def zs_copy(i):
        return remote(zs.at[z_rows(i)], zr.at[i - 1], zs_s.at[i - 1], zs_r.at[i - 1], z_peer[i - 1])

    for i in range(1, nz):
        zs_copy(i).start()
    own_b = 2 * y + c
    src_b = jnp.minimum(own_b, 3 * nb - 1)
    old_cols = pl.ds(pl.multiple_of(lax.rem(src_b, nb) * BLK, BLK), BLK)
    old_t[...] = w3[src_b // nb, :, old_cols].astype(F32).T
    old = old_t[z_rows(0), :]
    old_norm = jnp.sqrt(jnp.sum(old * old, axis=1, keepdims=True))
    updated = zs[z_rows(0), :]
    for i in range(1, nz):
        zs_copy(i).wait_recv()
        updated += zr[i - 1]
    updated += old
    squares = jnp.sum(updated * updated, axis=1, keepdims=True)
    fresh[own_b, z_rows(0), :] = (updated * (old_norm / jnp.sqrt(squares + NORM_EPS))).astype(BF16)

    def az_copy(i):
        here = fresh.at[own_b, z_rows(0)]
        return remote(here, here, az_s.at[i - 1], az_r.at[i - 1], z_peer[i - 1])

    for i in range(1, nz):
        az_copy(i).start()
    halo_wait(HOPS - 1)
    attend(HOPS, 0, heads // 2)
    for i in range(1, nz):
        az_copy(i).wait_recv()

    def ag_copy(way, part, hop):
        origin = toward(1 - way, hop)
        here = fresh.at[2 * origin + c, rows_of[part]]
        n = slot[way, part, hop]
        return remote(here, here, ag_s.at[n], ag_r.at[n], (y_next, y_prev)[way])

    def ag_arrival(way, part, hop):
        origin = toward(1 - way, hop + 1)
        here = fresh.at[2 * origin + c, rows_of[part]]
        n = slot[way, part, hop]
        return remote(here, here, ag_s.at[n], ag_r.at[n], (y_next, y_prev)[way])

    def ad_copy(n, origin, part):
        here = fresh.at[2 * origin + c, rows_of[part]]
        return remote(here, here, ad_s.at[n], ad_r.at[n], mate)

    for way, part in order:
        if chain[way, part] > 0:
            ag_copy(way, part, 0).start()
    passed = []
    for part in range(2):
        passed.append((y, part))
        ad_copy(len(passed) - 1, y, part).start()
    attend(HOPS, heads // 2, heads)
    for h in range(heads):
        cols = slice(h * HEAD_DIM, (h + 1) * HEAD_DIM)
        att_v[:, cols] = (acc_s[h] / l_s[h]).astype(BF16)
    att_out = pltpu.make_async_copy(att_v, att_h, osem.at[0])
    att_out.start()
    for hop in range(max_hop):
        for way, part in order:
            if hop >= chain[way, part]:
                continue
            ag_arrival(way, part, hop).wait_recv()
            if hop + 1 < chain[way, part]:
                ag_copy(way, part, hop + 1).start()
            origin = toward(1 - way, hop + 1)
            passed.append((origin, part))
            ad_copy(len(passed) - 1, origin, part).start()
    for n, (origin, part) in enumerate(passed):
        ad_copy(n, origin, part).wait_recv()

    loads[9].wait()
    hid = nb * BLK
    queries = fq[...]
    gate_q = contract_cols(queries, fresh[0:nb].reshape(hid, feat))
    up_q = contract_cols(queries, fresh[nb:2 * nb].reshape(hid, feat))
    hidden = (jax.nn.silu(gate_q) * up_q).astype(BF16)
    out_v[...] = jnp.dot(
        hidden, fresh[2 * nb:3 * nb].reshape(hid, feat), preferred_element_type=F32
    ).astype(BF16)
    fast_out = pltpu.make_async_copy(out_v, out_h, osem.at[1])
    fast_out.start()

    for step in range(HOPS):
        halo_send_wait(step)
    for part in range(2):
        pair_copy(part).wait_send()
    term_copy.wait_send()
    for way, part, hop in slot:
        rs_copy(way, part, hop).wait_send()
        ag_copy(way, part, hop).wait_send()
    for i in range(1, nz):
        zs_copy(i).wait_send()
        az_copy(i).wait_send()
    for n, (origin, part) in enumerate(passed):
        ad_copy(n, origin, part).wait_send()
    att_out.wait()
    fast_out.wait()


def solution(mesh):
    nz = 4 if mesh.shape["seq"] == 64 else 2
    ny = mesh.shape["seq"] // (2 * nz)

    def body(att_q, att_k, att_v, fast_q, fast_k, fast_v, rates, w_gate, w_up, w_down):
        tok, feat = att_q.shape
        hid = w_gate.shape[1]
        heads = feat // HEAD_DIM
        n_slot = 2 * (ny - 1)
        dma = pltpu.SemaphoreType.DMA
        vmem = pltpu.VMEM
        hbm = pl.BlockSpec(memory_space=pl.ANY)
        return pl.pallas_call(
            functools.partial(kernel, ny, nz),
            out_shape=(
                jax.ShapeDtypeStruct((tok, feat), BF16),
                jax.ShapeDtypeStruct((tok, feat), BF16),
            ),
            in_specs=[hbm] * 10,
            out_specs=(hbm, hbm),
            scratch_shapes=[
                vmem((tok, feat), BF16),
                vmem((2, tok, feat), BF16),
                vmem((HOPS, 2, tok, feat), BF16),
                vmem((tok, feat), BF16),
                vmem((2, 2, tok, feat), BF16),
                vmem((1, tok), F32),
                vmem((3, feat, hid), BF16),
                vmem((2, tok, ny * BLK), BF16),
                vmem((tok, ny * BLK), BF16),
                vmem((ny, BLK, feat), F32),
                vmem((n_slot, BLK // 2, feat), F32),
                vmem((BLK, feat), F32),
                vmem((nz - 1, BLK // nz, feat), F32),
                vmem((BLK, feat), F32),
                vmem((2 * ny, BLK, feat), BF16),
                vmem((heads, tok, 1), F32),
                vmem((heads, tok, 1), F32),
                vmem((heads, tok, HEAD_DIM), F32),
                vmem((tok, feat), BF16),
                vmem((tok, feat), BF16),
                dma((10,)),
                dma((2,)),
                dma((HOPS, 2)),
                dma((HOPS, 2)),
                dma((2,)),
                dma((2,)),
                dma,
                dma,
                dma((n_slot,)),
                dma((n_slot,)),
                dma((nz - 1,)),
                dma((nz - 1,)),
                dma((nz - 1,)),
                dma((nz - 1,)),
                dma((n_slot,)),
                dma((n_slot,)),
                dma((2 * ny,)),
                dma((2 * ny,)),
            ],
            compiler_params=pltpu.CompilerParams(
                collective_id=0, has_side_effects=True, vmem_limit_bytes=60 * 1024 * 1024
            ),
        )(
            att_q, att_k, att_v, fast_q, fast_k, fast_v, rates.reshape(1, -1),
            w_gate, w_up, w_down,
        )

    rows = P("seq", "head")
    weights = P(None, "head")
    return jax.shard_map(
        body,
        mesh=mesh,
        in_specs=(rows,) * 6 + (P("seq"),) + (weights,) * 3,
        out_specs=(rows, rows),
        check_vma=False,
    )
```

time: 313 us -> 101 us (0.32)
  the two profiles are of different devices: /device:TPU:475 before, /device:TPU:1 now
where the time goes in v1:
time: 101 us
  Pallas kernels  97.5 us (97%)
  local copies, waits for them, and re-layouts  2.5 us (2%)
    pallas_call x1, Pallas kernels, body(): pl.pallas_call(functools.partial(kernel, ny, nz), out_shape=(jax.ShapeDty...  97.5 us
    unnamed x4, local copies, waits for them, and re-layouts  2.5 us

profile of v1, /device:TPU:1, one launch (start us, length us, event | category | flops | bytes accessed | tf_op | source)
XLA Modules:
  0.0 100.6 jit_solution(17393651687795540935)
XLA Ops:
  0.6 97.5 %shard_map.113 = (bf16[256,640]{1,0:T(8,128)(2,1)}, bf16[256,640]{1,0:T(8,128)(2,1)}) custom-call(bf16[256,640]{1,0:T(8,128)(2,1)} %aq_h.1, bf16[256,640]{1,0:T(8,128)(2,1)} %ak_h.1, bf16[256,640]{1,0:T(8,128)(2,1)} %av_h.1, bf16[256,640]{1,0:T(8,128)(2,1)} %fq_h.1, bf16[256,640]{1,0:T(8,128)(2,1)} %fk_h.1, bf16[256,640]{1,0:T(8,128)(2,1)} %fv_h.1, ...), custom_call_target="tpu_custom_call" | custom-call | tf_op jit(solution)/shard_map/pallas_call | solution.py:358
  98.1 0.0 copy-start
  98.1 1.8 %copy.14 = bf16[256,640]{1,0:T(8,128)(2,1)} copy(bf16[256,640]{1,0:T(8,128)(2,1)} %get-tuple-element.4) | data formatting | bytes 655360
  99.9 0.0 copy-done
  99.9 0.7 copy.15
Async XLA Ops:
  98.1 1.8 %copy-start = (bf16[256,640]{1,0:T(8,128)(2,1)S(1)}, bf16[256,640]{1,0:T(8,128)(2,1)}, u32[]{:S(2)}) copy-start(bf16[256,640]{1,0:T(8,128)(2,1)} %get-tuple-element.5) | copy-start | bytes 983044

commit v2 on v1

--- a/solution.py
+++ b/solution.py
@@ -52,8 +52,9 @@
     y_next = z * 2 * ny + lax.rem(y + 1, ny) * 2 + c
     y_prev = z * 2 * ny + lax.rem(y + ny - 1, ny) * 2 + c
     z_peer = [lax.rem(z + i, nz) * 2 * ny + y * 2 + c for i in range(1, nz)]
-    chain = {(0, 0): ny // 2, (0, 1): ny // 2 - 1, (1, 0): ny // 2 - 1, (1, 1): ny // 2}
-    max_hop = ny // 2
+    lean = max(ny // 4, 1)
+    chain = {(0, 0): lean, (0, 1): lean + 1, (1, 0): ny - 1 - lean, (1, 1): ny - 2 - lean}
+    even = {(0, 0): ny // 2, (0, 1): ny // 2 - 1, (1, 0): ny // 2 - 1, (1, 1): ny // 2}
 
     def remote(src, dst, ssem, rsem, dev):
         return pltpu.make_async_remote_copy(
@@ -197,11 +198,13 @@
     grad[nb:ny] += contract_rows(rt[:, split:width], kvf[1, 1]).reshape(ny - nb, BLK, feat)
 
     rows_of = [pl.ds(0, half), pl.ds(half, half)]
-    slot = {}
+    slot, ag_slot = {}, {}
     for way in range(2):
         for part in range(2):
             for hop in range(chain[way, part]):
                 slot[way, part, hop] = len(slot)
+            for hop in range(even[way, part]):
+                ag_slot[way, part, hop] = len(ag_slot)
 
     def toward(way, dist):
         return lax.rem(y + dist, ny) if way == 0 else lax.rem(y + ny - dist, ny)
@@ -214,12 +217,23 @@
         n = slot[way, part, hop]
         return remote(src, ry.at[n], rs_s.at[n], rs_r.at[n], (y_next, y_prev)[way])
 
-    order = [(0, 0), (1, 1), (0, 1), (1, 0)]
+    @pl.when(c == 1)
+    def _():
+        halo_wait(0)
+        halo_send(1)
+
+    order = [(1, 0), (0, 1), (1, 1), (0, 0)]
     for way, part in order:
         if chain[way, part] > 0:
             rs_copy(way, part, 0).start()
     attend(0, heads // 2, heads)
-    for hop in range(max_hop):
+
+    @pl.when(c == 0)
+    def _():
+        halo_wait(0)
+        halo_send(1)
+
+    for hop in range(max(chain.values())):
         for way, part in order:
             if hop >= chain[way, part]:
                 continue
@@ -228,7 +242,9 @@
                 n = slot[way, part, hop]
                 ry[n] += grad[toward(way, chain[way, part] - hop - 1), rows_of[part]]
                 rs_copy(way, part, hop + 1).start()
-        if hop < HOPS - 1:
+        if hop == 0:
+            attend(1, 0, heads)
+        elif hop < HOPS - 1:
             halo_wait(hop)
             halo_send(hop + 1)
             attend(hop + 1, 0, heads)
@@ -275,21 +291,21 @@
     def ag_copy(way, part, hop):
         origin = toward(1 - way, hop)
         here = fresh.at[2 * origin + c, rows_of[part]]
-        n = slot[way, part, hop]
+        n = ag_slot[way, part, hop]
         return remote(here, here, ag_s.at[n], ag_r.at[n], (y_next, y_prev)[way])
 
     def ag_arrival(way, part, hop):
         origin = toward(1 - way, hop + 1)
         here = fresh.at[2 * origin + c, rows_of[part]]
-        n = slot[way, part, hop]
+        n = ag_slot[way, part, hop]
         return remote(here, here, ag_s.at[n], ag_r.at[n], (y_next, y_prev)[way])
 
     def ad_copy(n, origin, part):
         here = fresh.at[2 * origin + c, rows_of[part]]
         return remote(here, here, ad_s.at[n], ad_r.at[n], mate)
 
-    for way, part in order:
-        if chain[way, part] > 0:
+    for way, part in even:
+        if even[way, part] > 0:
             ag_copy(way, part, 0).start()
     passed = []
     for part in range(2):
@@ -301,12 +317,12 @@
         att_v[:, cols] = (acc_s[h] / l_s[h]).astype(BF16)
     att_out = pltpu.make_async_copy(att_v, att_h, osem.at[0])
     att_out.start()
-    for hop in range(max_hop):
-        for way, part in order:
-            if hop >= chain[way, part]:
+    for hop in range(ny // 2):
+        for way, part in even:
+            if hop >= even[way, part]:
                 continue
             ag_arrival(way, part, hop).wait_recv()
-            if hop + 1 < chain[way, part]:
+            if hop + 1 < even[way, part]:
                 ag_copy(way, part, hop + 1).start()
             origin = toward(1 - way, hop + 1)
             passed.append((origin, part))
@@ -333,6 +349,7 @@
     term_copy.wait_send()
     for way, part, hop in slot:
         rs_copy(way, part, hop).wait_send()
+    for way, part, hop in ag_slot:
         ag_copy(way, part, hop).wait_send()
     for i in range(1, nz):
         zs_copy(i).wait_send()

time: 101 us -> 96.2 us (0.952)
  Pallas kernels: 97.5 us -> 92.9 us
    pallas_call x1, Pallas kernels: 97.5 us -> 92.9 us  [body(): pl.pallas_call(functools.partial(kernel, ny, nz), out_shape=(jax.ShapeDty...]
where the time goes in v2:
time: 96.2 us; the launch traced here: 96.1 us
  Pallas kernels  92.9 us (97%)
  local copies, waits for them, and re-layouts  2.5 us (3%)
    pallas_call x1, Pallas kernels, body(): pl.pallas_call(functools.partial(kernel, ny, nz), out_shape=(jax.ShapeDty...  92.9 us
    unnamed x4, local copies, waits for them, and re-layouts  2.5 us

profile of v2, /device:TPU:1, one launch (start us, length us, event | category | flops | bytes accessed | tf_op | source)
XLA Modules:
  0.0 96.1 jit_solution(8773669055502324004)
XLA Ops:
  0.6 92.9 %shard_map.113 = (bf16[256,640]{1,0:T(8,128)(2,1)}, bf16[256,640]{1,0:T(8,128)(2,1)}) custom-call(bf16[256,640]{1,0:T(8,128)(2,1)} %aq_h.1, bf16[256,640]{1,0:T(8,128)(2,1)} %ak_h.1, bf16[256,640]{1,0:T(8,128)(2,1)} %av_h.1, bf16[256,640]{1,0:T(8,128)(2,1)} %fq_h.1, bf16[256,640]{1,0:T(8,128)(2,1)} %fk_h.1, bf16[256,640]{1,0:T(8,128)(2,1)} %fv_h.1, ...), custom_call_target="tpu_custom_call" | custom-call | tf_op jit(solution)/shard_map/pallas_call | solution.py:375
  93.5 0.0 copy-start
  93.6 1.8 %copy.14 = bf16[256,640]{1,0:T(8,128)(2,1)} copy(bf16[256,640]{1,0:T(8,128)(2,1)} %get-tuple-element.4) | data formatting | bytes 655360
  95.3 0.0 copy-done
  95.3 0.7 copy.15
Async XLA Ops:
  93.5 1.8 %copy-start = (bf16[256,640]{1,0:T(8,128)(2,1)S(1)}, bf16[256,640]{1,0:T(8,128)(2,1)}, u32[]{:S(2)}) copy-start(bf16[256,640]{1,0:T(8,128)(2,1)} %get-tuple-element.5) | copy-start | bytes 983044

commit v3 on v2

--- a/solution.py
+++ b/solution.py
@@ -10,6 +10,8 @@
 HEAD_DIM = 128
 BLK = 128
 HOPS = 4
+RS_Z = 256
+AG_Z = 128
 NORM_EPS = 1e-06
 MASKED = -1e30
 MESH = pl.DeviceIdType.MESH
@@ -31,12 +33,14 @@
 
 
 def kernel(
-    ny, nz,
+    ny, nz, rs_lanes, ag_lanes,
     aq_h, ak_h, av_h, fq_h, fk_h, fv_h, lr_h, wg_h, wu_h, wd_h,
     att_h, out_h,
     aq, okv, halo, fq, kvf, lr, w3, tt, rt, grad, ry, zs, zr, old_t, fresh,
+    g_z, gb_z, in_z, q_z, qb_z, in_y, fresh_z,
     m_s, l_s, acc_s, att_v, out_v,
     loc, osem, hs, hr, ps, pr, ts, tr, rs_s, rs_r, zs_s, zs_r, az_s, az_r, ag_s, ag_r, ad_s, ad_r,
+    zz_s, zz_r, zy_s, zy_r, by_s, by_r, bz_s, bz_r, bd_s, bd_r,
 ):
     tok, feat = aq.shape
     nb = w3.shape[2] // BLK
@@ -51,6 +55,7 @@
     mate = s + 1 - 2 * c
     y_next = z * 2 * ny + lax.rem(y + 1, ny) * 2 + c
     y_prev = z * 2 * ny + lax.rem(y + ny - 1, ny) * 2 + c
+    y_peer = [z * 2 * ny + lax.rem(y + k, ny) * 2 + c for k in range(1, ny)]
     z_peer = [lax.rem(z + i, nz) * 2 * ny + y * 2 + c for i in range(1, nz)]
     lean = max(ny // 4, 1)
     chain = {(0, 0): lean, (0, 1): lean + 1, (1, 0): ny - 1 - lean, (1, 1): ny - 2 - lean}
@@ -72,7 +77,7 @@
         one.start()
 
     barrier = pltpu.get_barrier_semaphore()
-    for peer in [mate, y_next, y_prev] + z_peer:
+    for peer in [mate] + y_peer + z_peer:
         pl.semaphore_signal(barrier, inc=1, device_id={"seq": peer}, device_id_type=MESH)
 
     @pl.when((c == 1) & (s < total - 1))
@@ -84,7 +89,7 @@
         pl.semaphore_signal(barrier, inc=1, device_id={"seq": s - 1}, device_id_type=MESH)
 
     beside = c * (1 - s // (total - 1)) + (1 - c) * ((s + total - 1) // total)
-    pl.semaphore_wait(barrier, 3 + len(z_peer) + beside)
+    pl.semaphore_wait(barrier, 1 + len(y_peer) + len(z_peer) + beside)
 
     def halo_copy(step, part, dev):
         if step == 0:
@@ -186,16 +191,58 @@
 
     split = nb * BLK
     width = ny * BLK
-    grad[0:nb] = contract_rows(tt[c, :, 0:split], kvf[0, 0]).reshape(nb, BLK, feat)
-    grad[nb:ny] = contract_rows(tt[c, :, split:width], kvf[0, 1]).reshape(ny - nb, BLK, feat)
+    lanes_y, lanes_z = pl.ds(0, rs_lanes), pl.ds(rs_lanes, feat - rs_lanes)
+
+    def add_grads(terms, side, lanes, into, first):
+        low = contract_rows(terms(0, split), kvf[side, 0, :, lanes]).reshape(nb, BLK, -1)
+        high = contract_rows(terms(split, width), kvf[side, 1, :, lanes]).reshape(ny - nb, BLK, -1)
+        if first:
+            into[0:nb], into[nb:ny] = low, high
+        else:
+            into[0:nb] += low
+            into[nb:ny] += high
+
+    def own_terms(lo, hi):
+        return tt[c, :, lo:hi]
+
+    def mate_terms(lo, hi):
+        return rt[:, lo:hi]
+
+    add_grads(own_terms, 0, lanes_z, g_z, True)
+    add_grads(own_terms, 0, lanes_y, grad, True)
     for i in range(6, 9):
         loads[i].wait()
-    attend(0, 0, heads // 2)
     term_copy.wait_recv()
     for part in range(2):
         pair_copy(part).wait_recv()
-    grad[0:nb] += contract_rows(rt[:, 0:split], kvf[1, 0]).reshape(nb, BLK, feat)
-    grad[nb:ny] += contract_rows(rt[:, split:width], kvf[1, 1]).reshape(ny - nb, BLK, feat)
+    add_grads(mate_terms, 1, lanes_z, g_z, False)
+
+    def z_rows(i):
+        return pl.ds(pl.multiple_of(lax.rem(z + i, nz) * zrow, zrow), zrow)
+
+    gb_z[...] = g_z[...].astype(BF16)
+
+    def zz_copy(i):
+        return remote(gb_z.at[:, z_rows(i)], in_z.at[i - 1], zz_s.at[i - 1], zz_r.at[i - 1], z_peer[i - 1])
+
+    def zy_copy(k):
+        return remote(
+            qb_z.at[lax.rem(y + k, ny)], in_y.at[k - 1], zy_s.at[k - 1], zy_r.at[k - 1], y_peer[k - 1]
+        )
+
+    for i in range(1, nz):
+        zz_copy(i).start()
+    add_grads(mate_terms, 1, lanes_y, grad, False)
+
+    def turn_z():
+        got = g_z[:, z_rows(0), :]
+        for i in range(1, nz):
+            zz_copy(i).wait_recv()
+            got += in_z[i - 1].astype(F32)
+        q_z[...] = got
+        qb_z[...] = got.astype(BF16)
+        for k in range(1, ny):
+            zy_copy(k).start()
 
     rows_of = [pl.ds(0, half), pl.ds(half, half)]
     slot, ag_slot = {}, {}
@@ -226,7 +273,7 @@
     for way, part in order:
         if chain[way, part] > 0:
             rs_copy(way, part, 0).start()
-    attend(0, heads // 2, heads)
+    attend(0, 0, heads)
 
     @pl.when(c == 0)
     def _():
@@ -242,6 +289,8 @@
                 n = slot[way, part, hop]
                 ry[n] += grad[toward(way, chain[way, part] - hop - 1), rows_of[part]]
                 rs_copy(way, part, hop + 1).start()
+        if hop == min(2, max(chain.values()) - 1):
+            turn_z()
         if hop == 0:
             attend(1, 0, heads)
         elif hop < HOPS - 1:
@@ -255,9 +304,6 @@
                 got += ry[slot[way, part, chain[way, part] - 1]]
         zs[rows_of[part]] = got
 
-    def z_rows(i):
-        return pl.ds(pl.multiple_of(lax.rem(z + i, nz) * zrow, zrow), zrow)
-
     def zs_copy(i):
         return remote(zs.at[z_rows(i)], zr.at[i - 1], zs_s.at[i - 1], zs_r.at[i - 1], z_peer[i - 1])
 
@@ -269,39 +315,57 @@
     old_t[...] = w3[src_b // nb, :, old_cols].astype(F32).T
     old = old_t[z_rows(0), :]
     old_norm = jnp.sqrt(jnp.sum(old * old, axis=1, keepdims=True))
-    updated = zs[z_rows(0), :]
+    sum_z = q_z[y]
+    for k in range(1, ny):
+        zy_copy(k).wait_recv()
+        sum_z += in_y[k - 1].astype(F32)
+    sum_y = zs[z_rows(0), :]
     for i in range(1, nz):
         zs_copy(i).wait_recv()
-        updated += zr[i - 1]
-    updated += old
+        sum_y += zr[i - 1]
+    updated = old + jnp.concatenate([sum_y, sum_z], axis=1)
     squares = jnp.sum(updated * updated, axis=1, keepdims=True)
-    fresh[own_b, z_rows(0), :] = (updated * (old_norm / jnp.sqrt(squares + NORM_EPS))).astype(BF16)
-
-    def az_copy(i):
-        here = fresh.at[own_b, z_rows(0)]
+    new = (updated * (old_norm / jnp.sqrt(squares + NORM_EPS))).astype(BF16)
+    fresh[c, y, z_rows(0), :] = new[:, :ag_lanes]
+    fresh_z[c, y, z_rows(0), :] = new[:, ag_lanes:]
+
+    def by_copy(k, arrival):
+        here = fresh_z.at[c, lax.rem(y + ny - k, ny) if arrival else y, z_rows(0)]
+        return remote(here, here, by_s.at[k - 1], by_r.at[k - 1], y_peer[k - 1])
+
+    def bz_copy(i, arrival):
+        here = fresh_z.at[c, :, z_rows(nz - i) if arrival else z_rows(0)]
+        return remote(here, here, bz_s.at[i - 1], bz_r.at[i - 1], z_peer[i - 1])
+
+    def bd_copy(i, arrival):
+        here = fresh_z.at[1 - c if arrival else c, :, z_rows(nz - i)]
+        return remote(here, here, bd_s.at[i], bd_r.at[i], mate)
+
+    def az_copy(i, arrival):
+        here = fresh.at[c, y, z_rows(nz - i) if arrival else z_rows(0)]
         return remote(here, here, az_s.at[i - 1], az_r.at[i - 1], z_peer[i - 1])
 
     for i in range(1, nz):
-        az_copy(i).start()
-    halo_wait(HOPS - 1)
-    attend(HOPS, 0, heads // 2)
-    for i in range(1, nz):
-        az_copy(i).wait_recv()
+        az_copy(i, False).start()
+    for k in range(1, ny):
+        by_copy(k, False).start()
+    for i in range(1, nz):
+        az_copy(i, True).wait_recv()
 
     def ag_copy(way, part, hop):
         origin = toward(1 - way, hop)
-        here = fresh.at[2 * origin + c, rows_of[part]]
+        here = fresh.at[c, origin, rows_of[part]]
         n = ag_slot[way, part, hop]
         return remote(here, here, ag_s.at[n], ag_r.at[n], (y_next, y_prev)[way])
 
     def ag_arrival(way, part, hop):
         origin = toward(1 - way, hop + 1)
-        here = fresh.at[2 * origin + c, rows_of[part]]
+        here = fresh.at[c, origin, rows_of[part]]
         n = ag_slot[way, part, hop]
         return remote(here, here, ag_s.at[n], ag_r.at[n], (y_next, y_prev)[way])
 
-    def ad_copy(n, origin, part):
-        here = fresh.at[2 * origin + c, rows_of[part]]
+    def ad_copy(n, origin, part, arrival):
+        here = fresh.at[1 - c if arrival else c, origin, rows_of[part]]
         return remote(here, here, ad_s.at[n], ad_r.at[n], mate)
 
     for way, part in even:
@@ -310,8 +374,14 @@
     passed = []
     for part in range(2):
         passed.append((y, part))
-        ad_copy(len(passed) - 1, y, part).start()
-    attend(HOPS, heads // 2, heads)
+        ad_copy(len(passed) - 1, y, part, False).start()
+    for k in range(1, ny):
+        by_copy(k, True).wait_recv()
+    for i in range(1, nz):
+        bz_copy(i, False).start()
+    bd_copy(0, False).start()
+    halo_wait(HOPS - 1)
+    attend(HOPS, 0, heads)
     for h in range(heads):
         cols = slice(h * HEAD_DIM, (h + 1) * HEAD_DIM)
         att_v[:, cols] = (acc_s[h] / l_s[h]).astype(BF16)
@@ -326,19 +396,32 @@
                 ag_copy(way, part, hop + 1).start()
             origin = toward(1 - way, hop + 1)
             passed.append((origin, part))
-            ad_copy(len(passed) - 1, origin, part).start()
+            ad_copy(len(passed) - 1, origin, part, False).start()
+        if hop == ny // 2 - 2:
+            for i in range(1, nz):
+                bz_copy(i, True).wait_recv()
+                bd_copy(i, False).start()
+    for i in range(nz):
+        bd_copy(i, True).wait_recv()
     for n, (origin, part) in enumerate(passed):
-        ad_copy(n, origin, part).wait_recv()
+        ad_copy(n, origin, part, True).wait_recv()
 
     loads[9].wait()
-    hid = nb * BLK
-    queries = fq[...]
-    gate_q = contract_cols(queries, fresh[0:nb].reshape(hid, feat))
-    up_q = contract_cols(queries, fresh[nb:2 * nb].reshape(hid, feat))
-    hidden = (jax.nn.silu(gate_q) * up_q).astype(BF16)
-    out_v[...] = jnp.dot(
-        hidden, fresh[2 * nb:3 * nb].reshape(hid, feat), preferred_element_type=F32
-    ).astype(BF16)
+    queries_y, queries_z = fq[:, :ag_lanes], fq[:, ag_lanes:]
+
+    def weights(ref, which):
+        return jnp.concatenate(
+            [ref[b % 2, b // 2] for b in range(which * nb, (which + 1) * nb)], axis=0
+        )
+
+    def project(which):
+        return contract_cols(queries_y, weights(fresh, which)) + contract_cols(
+            queries_z, weights(fresh_z, which)
+        )
+
+    hidden = (jax.nn.silu(project(0)) * project(1)).astype(BF16)
+    out_v[:, :ag_lanes] = jnp.dot(hidden, weights(fresh, 2), preferred_element_type=F32).astype(BF16)
+    out_v[:, ag_lanes:] = jnp.dot(hidden, weights(fresh_z, 2), preferred_element_type=F32).astype(BF16)
     fast_out = pltpu.make_async_copy(out_v, out_h, osem.at[1])
     fast_out.start()
 
@@ -353,9 +436,16 @@
         ag_copy(way, part, hop).wait_send()
     for i in range(1, nz):
         zs_copy(i).wait_send()
-        az_copy(i).wait_send()
+        az_copy(i, False).wait_send()
+        zz_copy(i).wait_send()
+        bz_copy(i, False).wait_send()
+    for k in range(1, ny):
+        zy_copy(k).wait_send()
+        by_copy(k, False).wait_send()
+    for i in range(nz):
+        bd_copy(i, False).wait_send()
     for n, (origin, part) in enumerate(passed):
-        ad_copy(n, origin, part).wait_send()
+        ad_copy(n, origin, part, False).wait_send()
     att_out.wait()
     fast_out.wait()
 
@@ -369,11 +459,13 @@
         hid = w_gate.shape[1]
         heads = feat // HEAD_DIM
         n_slot = 2 * (ny - 1)
+        rs_lanes, ag_lanes = feat - RS_Z, feat - AG_Z
+        zrow = BLK // nz
         dma = pltpu.SemaphoreType.DMA
         vmem = pltpu.VMEM
         hbm = pl.BlockSpec(memory_space=pl.ANY)
         return pl.pallas_call(
-            functools.partial(kernel, ny, nz),
+            functools.partial(kernel, ny, nz, rs_lanes, ag_lanes),
             out_shape=(
                 jax.ShapeDtypeStruct((tok, feat), BF16),
                 jax.ShapeDtypeStruct((tok, feat), BF16),
@@ -390,12 +482,19 @@
                 vmem((3, feat, hid), BF16),
                 vmem((2, tok, ny * BLK), BF16),
                 vmem((tok, ny * BLK), BF16),
-                vmem((ny, BLK, feat), F32),
-                vmem((n_slot, BLK // 2, feat), F32),
+                vmem((ny, BLK, rs_lanes), F32),
+                vmem((n_slot, BLK // 2, rs_lanes), F32),
+                vmem((BLK, rs_lanes), F32),
+                vmem((nz - 1, zrow, rs_lanes), F32),
                 vmem((BLK, feat), F32),
-                vmem((nz - 1, BLK // nz, feat), F32),
-                vmem((BLK, feat), F32),
-                vmem((2 * ny, BLK, feat), BF16),
+                vmem((2, ny, BLK, ag_lanes), BF16),
+                vmem((ny, BLK, RS_Z), F32),
+                vmem((ny, BLK, RS_Z), BF16),
+                vmem((nz - 1, ny, zrow, RS_Z), BF16),
+                vmem((ny, zrow, RS_Z), F32),
+                vmem((ny, zrow, RS_Z), BF16),
+                vmem((ny - 1, zrow, RS_Z), BF16),
+                vmem((2, ny, BLK, AG_Z), BF16),
                 vmem((heads, tok, 1), F32),
                 vmem((heads, tok, 1), F32),
                 vmem((heads, tok, HEAD_DIM), F32),
@@ -419,6 +518,16 @@
                 dma((n_slot,)),
                 dma((2 * ny,)),
                 dma((2 * ny,)),
+                dma((nz - 1,)),
+                dma((nz - 1,)),
+                dma((ny - 1,)),
+                dma((ny - 1,)),
+                dma((ny - 1,)),
+                dma((ny - 1,)),
+                dma((nz - 1,)),
+                dma((nz - 1,)),
+                dma((nz,)),
+                dma((nz,)),
             ],
             compiler_params=pltpu.CompilerParams(
                 collective_id=0, has_side_effects=True, vmem_limit_bytes=60 * 1024 * 1024

time: 96.2 us -> 87.8 us (0.913)
  Pallas kernels: 92.9 us -> 84.5 us
    pallas_call x1, Pallas kernels: 92.9 us -> 84.5 us  [body(): pl.pallas_call(functools.partial(kernel, ny, nz, rs_lanes, ag_lanes), out...]
where the time goes in v3:
time: 87.8 us; the launch traced here: 87.7 us
  Pallas kernels  84.5 us (96%)
  local copies, waits for them, and re-layouts  2.5 us (3%)
    pallas_call x1, Pallas kernels, body(): pl.pallas_call(functools.partial(kernel, ny, nz, rs_lanes, ag_lanes), out...  84.5 us
    unnamed x4, local copies, waits for them, and re-layouts  2.5 us

profile of v3, /device:TPU:1, one launch (start us, length us, event | category | flops | bytes accessed | tf_op | source)
XLA Modules:
  0.0 87.7 jit_solution(4989676978280577699)
XLA Ops:
  0.6 84.5 %shard_map.113 = (bf16[256,640]{1,0:T(8,128)(2,1)}, bf16[256,640]{1,0:T(8,128)(2,1)}) custom-call(bf16[256,640]{1,0:T(8,128)(2,1)} %aq_h.1, bf16[256,640]{1,0:T(8,128)(2,1)} %ak_h.1, bf16[256,640]{1,0:T(8,128)(2,1)} %av_h.1, bf16[256,640]{1,0:T(8,128)(2,1)} %fq_h.1, bf16[256,640]{1,0:T(8,128)(2,1)} %fk_h.1, bf16[256,640]{1,0:T(8,128)(2,1)} %fv_h.1, ...), custom_call_target="tpu_custom_call" | custom-call | tf_op jit(solution)/shard_map/pallas_call | solution.py:467
  85.2 0.0 copy-start
  85.2 1.8 %copy.14 = bf16[256,640]{1,0:T(8,128)(2,1)} copy(bf16[256,640]{1,0:T(8,128)(2,1)} %get-tuple-element.4) | data formatting | bytes 655360
  87.0 0.0 copy-done
  87.0 0.7 copy.15
Async XLA Ops:
  85.2 1.8 %copy-start = (bf16[256,640]{1,0:T(8,128)(2,1)S(1)}, bf16[256,640]{1,0:T(8,128)(2,1)}, u32[]{:S(2)}) copy-start(bf16[256,640]{1,0:T(8,128)(2,1)} %get-tuple-element.5) | copy-start | bytes 983044

commit v4 on v3

--- a/solution.py
+++ b/solution.py
@@ -57,9 +57,8 @@
     y_prev = z * 2 * ny + lax.rem(y + ny - 1, ny) * 2 + c
     y_peer = [z * 2 * ny + lax.rem(y + k, ny) * 2 + c for k in range(1, ny)]
     z_peer = [lax.rem(z + i, nz) * 2 * ny + y * 2 + c for i in range(1, nz)]
-    lean = max(ny // 4, 1)
-    chain = {(0, 0): lean, (0, 1): lean + 1, (1, 0): ny - 1 - lean, (1, 1): ny - 2 - lean}
-    even = {(0, 0): ny // 2, (0, 1): ny // 2 - 1, (1, 0): ny // 2 - 1, (1, 1): ny // 2}
+    chain = {(1, 0): ny // 2, (1, 1): ny // 2, (0, 0): ny // 2 - 1, (0, 1): ny // 2 - 1}
+    even = chain
 
     def remote(src, dst, ssem, rsem, dev):
         return pltpu.make_async_remote_copy(
@@ -89,7 +88,6 @@
         pl.semaphore_signal(barrier, inc=1, device_id={"seq": s - 1}, device_id_type=MESH)
 
     beside = c * (1 - s // (total - 1)) + (1 - c) * ((s + total - 1) // total)
-    pl.semaphore_wait(barrier, 1 + len(y_peer) + len(z_peer) + beside)
 
     def halo_copy(step, part, dev):
         if step == 0:
@@ -119,9 +117,17 @@
     def pair_copy(part):
         return remote((fk_h, fv_h)[part], kvf.at[1, part], ps.at[part], pr.at[part], mate)
 
-    for part in range(2):
-        pair_copy(part).start()
-    halo_send(0)
+    edge = 2 * y + c == 2 * ny - 1
+
+    def halo_turn(step, core, at_edge=None):
+        due = c == core
+        if at_edge is not None:
+            due = edge if at_edge else due & jnp.logical_not(edge)
+
+        @pl.when(due)
+        def _():
+            halo_wait(step - 1)
+            halo_send(step)
 
     scale = HEAD_DIM ** (-0.5)
 
@@ -186,8 +192,12 @@
         put(i, rb * pu * slope)
         put(nb + i, rb * silu)
         put(2 * nb + i, rate * silu * pu)
+    pl.semaphore_wait(barrier, 1 + len(y_peer) + len(z_peer) + beside)
+    for part in range(2):
+        pair_copy(part).start()
     term_copy = remote(tt.at[1 - c], rt, ts, tr, mate)
     term_copy.start()
+    halo_send(0)
 
     split = nb * BLK
     width = ny * BLK
@@ -212,6 +222,7 @@
     add_grads(own_terms, 0, lanes_y, grad, True)
     for i in range(6, 9):
         loads[i].wait()
+    attend(0, 0, 1)
     term_copy.wait_recv()
     for part in range(2):
         pair_copy(part).wait_recv()
@@ -264,39 +275,39 @@
         n = slot[way, part, hop]
         return remote(src, ry.at[n], rs_s.at[n], rs_r.at[n], (y_next, y_prev)[way])
 
-    @pl.when(c == 1)
-    def _():
-        halo_wait(0)
-        halo_send(1)
-
-    order = [(1, 0), (0, 1), (1, 1), (0, 0)]
-    for way, part in order:
-        if chain[way, part] > 0:
-            rs_copy(way, part, 0).start()
-    attend(0, 0, heads)
-
-    @pl.when(c == 0)
-    def _():
-        halo_wait(0)
-        halo_send(1)
-
-    for hop in range(max(chain.values())):
-        for way, part in order:
-            if hop >= chain[way, part]:
-                continue
+    for way, part in chain:
+        rs_copy(way, part, 0).start()
+    attend(0, 1, 3)
+
+    def rs_step(way, hop):
+        for part in range(2):
             rs_copy(way, part, hop).wait_recv()
             if hop + 1 < chain[way, part]:
                 n = slot[way, part, hop]
                 ry[n] += grad[toward(way, chain[way, part] - hop - 1), rows_of[part]]
                 rs_copy(way, part, hop + 1).start()
-        if hop == min(2, max(chain.values()) - 1):
-            turn_z()
-        if hop == 0:
-            attend(1, 0, heads)
-        elif hop < HOPS - 1:
-            halo_wait(hop)
-            halo_send(hop + 1)
-            attend(hop + 1, 0, heads)
+
+    rs_step(1, 0)
+    attend(0, 3, heads)
+    rs_step(0, 0)
+    rs_step(1, 1)
+    halo_wait(0)
+
+    @pl.when(c == 0)
+    def _():
+        halo_send(1)
+
+    rs_step(0, 1)
+    attend(1, 0, 2)
+    rs_step(1, 2)
+    turn_z()
+
+    @pl.when(c == 1)
+    def _():
+        halo_send(1)
+
+    rs_step(0, 2)
+    rs_step(1, 3)
     for part in range(2):
         got = grad[y, rows_of[part]]
         for way in range(2):
@@ -315,6 +326,8 @@
     old_t[...] = w3[src_b // nb, :, old_cols].astype(F32).T
     old = old_t[z_rows(0), :]
     old_norm = jnp.sqrt(jnp.sum(old * old, axis=1, keepdims=True))
+    halo_turn(2, 1, False)
+    attend(1, 2, heads)
     sum_z = q_z[y]
     for k in range(1, ny):
         zy_copy(k).wait_recv()
@@ -349,6 +362,9 @@
         az_copy(i, False).start()
     for k in range(1, ny):
         by_copy(k, False).start()
+    halo_turn(2, 1, True)
+    halo_turn(2, 0)
+    attend(2, 0, 3)
     for i in range(1, nz):
         az_copy(i, True).wait_recv()
 
@@ -375,18 +391,7 @@
     for part in range(2):
         passed.append((y, part))
         ad_copy(len(passed) - 1, y, part, False).start()
-    for k in range(1, ny):
-        by_copy(k, True).wait_recv()
-    for i in range(1, nz):
-        bz_copy(i, False).start()
-    bd_copy(0, False).start()
-    halo_wait(HOPS - 1)
-    attend(HOPS, 0, heads)
-    for h in range(heads):
-        cols = slice(h * HEAD_DIM, (h + 1) * HEAD_DIM)
-        att_v[:, cols] = (acc_s[h] / l_s[h]).astype(BF16)
-    att_out = pltpu.make_async_copy(att_v, att_h, osem.at[0])
-    att_out.start()
+    attend(2, 3, heads)
     for hop in range(ny // 2):
         for way, part in even:
             if hop >= even[way, part]:
@@ -401,6 +406,25 @@
             for i in range(1, nz):
                 bz_copy(i, True).wait_recv()
                 bd_copy(i, False).start()
+        if hop == 0:
+            for k in range(1, ny):
+                by_copy(k, True).wait_recv()
+            for i in range(1, nz):
+                bz_copy(i, False).start()
+            bd_copy(0, False).start()
+        if hop == 1:
+            halo_turn(3, 1)
+            halo_turn(3, 0)
+            attend(3, 0, 3)
+        if hop == 2:
+            attend(3, 3, heads)
+    halo_wait(HOPS - 1)
+    attend(HOPS, 0, heads)
+    for h in range(heads):
+        cols = slice(h * HEAD_DIM, (h + 1) * HEAD_DIM)
+        att_v[:, cols] = (acc_s[h] / l_s[h]).astype(BF16)
+    att_out = pltpu.make_async_copy(att_v, att_h, osem.at[0])
+    att_out.start()
     for i in range(nz):
         bd_copy(i, True).wait_recv()
     for n, (origin, part) in enumerate(passed):

time: 87.8 us -> 83.9 us (0.956)
  the two profiles are of different devices: /device:TPU:1 before, /device:TPU:70 now
where the time goes in v4:
time: 83.9 us; the launch traced here: 83.7 us
  Pallas kernels  80.6 us (96%)
  local copies, waits for them, and re-layouts  2.5 us (3%)
    pallas_call x1, Pallas kernels, body(): pl.pallas_call(functools.partial(kernel, ny, nz, rs_lanes, ag_lanes), out...  80.6 us
    unnamed x4, local copies, waits for them, and re-layouts  2.5 us

profile of v4, /device:TPU:70, one launch (start us, length us, event | category | flops | bytes accessed | tf_op | source)
XLA Modules:
  0.0 83.7 jit_solution(7083863295790667225)
XLA Ops:
  0.6 80.6 %shard_map.113 = (bf16[256,640]{1,0:T(8,128)(2,1)}, bf16[256,640]{1,0:T(8,128)(2,1)}) custom-call(bf16[256,640]{1,0:T(8,128)(2,1)} %aq_h.1, bf16[256,640]{1,0:T(8,128)(2,1)} %ak_h.1, bf16[256,640]{1,0:T(8,128)(2,1)} %av_h.1, bf16[256,640]{1,0:T(8,128)(2,1)} %fq_h.1, bf16[256,640]{1,0:T(8,128)(2,1)} %fk_h.1, bf16[256,640]{1,0:T(8,128)(2,1)} %fv_h.1, ...), custom_call_target="tpu_custom_call" | custom-call | tf_op jit(solution)/shard_map/pallas_call | solution.py:491
  81.2 0.0 copy-start
  81.2 1.8 %copy.14 = bf16[256,640]{1,0:T(8,128)(2,1)} copy(bf16[256,640]{1,0:T(8,128)(2,1)} %get-tuple-element.4) | data formatting | bytes 655360
  83.0 0.0 copy-done
  83.0 0.7 copy.15
Async XLA Ops:
  81.2 1.8 %copy-start = (bf16[256,640]{1,0:T(8,128)(2,1)S(1)}, bf16[256,640]{1,0:T(8,128)(2,1)}, u32[]{:S(2)}) copy-start(bf16[256,640]{1,0:T(8,128)(2,1)} %get-tuple-element.5) | copy-start | bytes 983044

commit v5 on v4

--- a/solution.py
+++ b/solution.py
@@ -13,6 +13,7 @@
 RS_Z = 256
 AG_Z = 128
 NORM_EPS = 1e-06
+LOG2_E = 1.4426950408889634
 MASKED = -1e30
 MESH = pl.DeviceIdType.MESH
 F32 = jnp.float32
@@ -35,11 +36,11 @@
 def kernel(
     ny, nz, rs_lanes, ag_lanes,
     aq_h, ak_h, av_h, fq_h, fk_h, fv_h, lr_h, wg_h, wu_h, wd_h,
-    att_h, out_h,
+    att_v, out_v,
     aq, okv, halo, fq, kvf, lr, w3, tt, rt, grad, ry, zs, zr, old_t, fresh,
     g_z, gb_z, in_z, q_z, qb_z, in_y, fresh_z,
-    m_s, l_s, acc_s, att_v, out_v,
-    loc, osem, hs, hr, ps, pr, ts, tr, rs_s, rs_r, zs_s, zs_r, az_s, az_r, ag_s, ag_r, ad_s, ad_r,
+    m_s, l_s, acc_s,
+    loc, hs, hr, ps, pr, ts, tr, rs_s, rs_r, zs_s, zs_r, az_s, az_r, ag_s, ag_r, ad_s, ad_r,
     zz_s, zz_r, zy_s, zy_r, by_s, by_r, bz_s, bz_r, bd_s, bd_r,
 ):
     tok, feat = aq.shape
@@ -87,7 +88,18 @@
     def _():
         pl.semaphore_signal(barrier, inc=1, device_id={"seq": s - 1}, device_id_type=MESH)
 
-    beside = c * (1 - s // (total - 1)) + (1 - c) * ((s + total - 1) // total)
+    @pl.when((c == 0) & (y == 0) & (z > 0))
+    def _():
+        pl.semaphore_signal(barrier, inc=1, device_id={"seq": s - 2}, device_id_type=MESH)
+
+    beside = (1 - c) * (y // (ny - 1)) * (1 - z // (nz - 1)) + c * (1 - s // (total - 1)) + (1 - c) * ((s + total - 1) // total)
+
+    place = 2 * y + c
+    edge = place == 2 * ny - 1
+    straight = (place == 2 * ny - 2) & (z < nz - 1)
+
+    def straight_copy(part):
+        return remote((ak_h, av_h)[part], halo.at[1, part], hs.at[HOPS, part], hr.at[1, part], s + 2)
 
     def halo_copy(step, part, dev):
         if step == 0:
@@ -96,14 +108,18 @@
             src = halo.at[step - 1, part]
         return remote(src, halo.at[step, part], hs.at[step, part], hr.at[step, part], dev)
 
+    def sends(step):
+        due = (s < total - 1) & (s >= step)
+        return due & jnp.logical_not(edge) if step == 1 else due
+
     def halo_send(step):
-        @pl.when((s < total - 1) & (s >= step))
+        @pl.when(sends(step))
         def _():
             for part in range(2):
                 halo_copy(step, part, s + 1).start()
 
     def halo_send_wait(step):
-        @pl.when((s < total - 1) & (s >= step))
+        @pl.when(sends(step))
         def _():
             for part in range(2):
                 halo_copy(step, part, s + 1).wait_send()
@@ -117,8 +133,6 @@
     def pair_copy(part):
         return remote((fk_h, fv_h)[part], kvf.at[1, part], ps.at[part], pr.at[part], mate)
 
-    edge = 2 * y + c == 2 * ny - 1
-
     def halo_turn(step, core, at_edge=None):
         due = c == core
         if at_edge is not None:
@@ -129,14 +143,17 @@
             halo_wait(step - 1)
             halo_send(step)
 
-    scale = HEAD_DIM ** (-0.5)
+    scale = HEAD_DIM ** (-0.5) * LOG2_E
+
+    def alone(fn):
+        pl.when(s >= 0)(fn)
 
     def attend(delta, lo, hi):
-        def one_head(h, _):
-            cols = pl.ds(pl.multiple_of(h * HEAD_DIM, HEAD_DIM), HEAD_DIM)
+        def one_head(h):
+            cols = slice(h * HEAD_DIM, (h + 1) * HEAD_DIM)
             kv = okv if delta == 0 else halo.at[delta - 1]
             key, val = kv[0, :, cols], kv[1, :, cols]
-            sc = contract_cols(aq[:, cols], key) * scale
+            sc = contract_cols(aq[:, cols], key)
             if delta in (0, HOPS):
                 qi = lax.broadcasted_iota(jnp.int32, (tok, tok), 0)
                 ki = lax.broadcasted_iota(jnp.int32, (tok, tok), 1)
@@ -144,26 +161,29 @@
                 sc = jnp.where(keep, sc, MASKED)
             top = jnp.max(sc, axis=1, keepdims=True)
             if delta == 0:
-                p = jnp.exp(sc - top)
+                p = jnp.exp2((sc - top) * scale)
                 m_s[h] = top
                 l_s[h] = jnp.sum(p, axis=1, keepdims=True)
                 acc_s[h] = jnp.dot(p.astype(BF16), val, preferred_element_type=F32)
             else:
                 m_old = m_s[h]
                 m_new = jnp.maximum(m_old, top)
-                p = jnp.exp(sc - m_new)
-                alpha = jnp.exp(m_old - m_new)
+                p = jnp.exp2((sc - m_new) * scale)
+                alpha = jnp.exp2((m_old - m_new) * scale)
                 m_s[h] = m_new
                 l_s[h] = l_s[h] * alpha + jnp.sum(p, axis=1, keepdims=True)
                 acc_s[h] = acc_s[h] * alpha + jnp.dot(p.astype(BF16), val, preferred_element_type=F32)
-            return 0
 
         if delta == 0:
-            lax.fori_loop(lo, hi, one_head, 0)
+            @alone
+            def _():
+                for h in range(lo, hi):
+                    one_head(h)
         else:
             @pl.when(s >= delta)
             def _():
-                lax.fori_loop(lo, hi, one_head, 0)
+                for h in range(lo, hi):
+                    one_head(h)
 
     loads[0].wait()
     loads[1].wait()
@@ -199,6 +219,12 @@
     term_copy.start()
     halo_send(0)
 
+    @pl.when(straight)
+    def _():
+        for part in range(2):
+            straight_copy(part).start()
+
+
     split = nb * BLK
     width = ny * BLK
     lanes_y, lanes_z = pl.ds(0, rs_lanes), pl.ds(rs_lanes, feat - rs_lanes)
@@ -218,15 +244,21 @@
     def mate_terms(lo, hi):
         return rt[:, lo:hi]
 
-    add_grads(own_terms, 0, lanes_z, g_z, True)
-    add_grads(own_terms, 0, lanes_y, grad, True)
+    @alone
+    def _():
+        add_grads(own_terms, 0, lanes_z, g_z, True)
+        add_grads(own_terms, 0, lanes_y, grad, True)
+
     for i in range(6, 9):
         loads[i].wait()
     attend(0, 0, 1)
     term_copy.wait_recv()
     for part in range(2):
         pair_copy(part).wait_recv()
-    add_grads(mate_terms, 1, lanes_z, g_z, False)
+    @alone
+    def _():
+        add_grads(mate_terms, 1, lanes_z, g_z, False)
+
 
     def z_rows(i):
         return pl.ds(pl.multiple_of(lax.rem(z + i, nz) * zrow, zrow), zrow)
@@ -243,7 +275,10 @@
 
     for i in range(1, nz):
         zz_copy(i).start()
-    add_grads(mate_terms, 1, lanes_y, grad, False)
+    @alone
+    def _():
+        add_grads(mate_terms, 1, lanes_y, grad, False)
+
 
     def turn_z():
         got = g_z[:, z_rows(0), :]
@@ -391,7 +426,6 @@
     for part in range(2):
         passed.append((y, part))
         ad_copy(len(passed) - 1, y, part, False).start()
-    attend(2, 3, heads)
     for hop in range(ny // 2):
         for way, part in even:
             if hop >= even[way, part]:
@@ -402,29 +436,27 @@
             origin = toward(1 - way, hop + 1)
             passed.append((origin, part))
             ad_copy(len(passed) - 1, origin, part, False).start()
-        if hop == ny // 2 - 2:
+        if hop == ny // 2 - 1:
             for i in range(1, nz):
                 bz_copy(i, True).wait_recv()
                 bd_copy(i, False).start()
         if hop == 0:
+            attend(2, 3, heads)
+        if hop == 1:
             for k in range(1, ny):
                 by_copy(k, True).wait_recv()
             for i in range(1, nz):
                 bz_copy(i, False).start()
             bd_copy(0, False).start()
-        if hop == 1:
             halo_turn(3, 1)
+        if hop == 2:
             halo_turn(3, 0)
-            attend(3, 0, 3)
-        if hop == 2:
-            attend(3, 3, heads)
+            attend(3, 0, heads)
     halo_wait(HOPS - 1)
     attend(HOPS, 0, heads)
     for h in range(heads):
         cols = slice(h * HEAD_DIM, (h + 1) * HEAD_DIM)
         att_v[:, cols] = (acc_s[h] / l_s[h]).astype(BF16)
-    att_out = pltpu.make_async_copy(att_v, att_h, osem.at[0])
-    att_out.start()
     for i in range(nz):
         bd_copy(i, True).wait_recv()
     for n, (origin, part) in enumerate(passed):
@@ -446,11 +478,15 @@
     hidden = (jax.nn.silu(project(0)) * project(1)).astype(BF16)
     out_v[:, :ag_lanes] = jnp.dot(hidden, weights(fresh, 2), preferred_element_type=F32).astype(BF16)
     out_v[:, ag_lanes:] = jnp.dot(hidden, weights(fresh_z, 2), preferred_element_type=F32).astype(BF16)
-    fast_out = pltpu.make_async_copy(out_v, out_h, osem.at[1])
-    fast_out.start()
 
     for step in range(HOPS):
         halo_send_wait(step)
+
+    @pl.when(straight)
+    def _():
+        for part in range(2):
+            straight_copy(part).wait_send()
+
     for part in range(2):
         pair_copy(part).wait_send()
     term_copy.wait_send()
@@ -470,8 +506,6 @@
         bd_copy(i, False).wait_send()
     for n, (origin, part) in enumerate(passed):
         ad_copy(n, origin, part, False).wait_send()
-    att_out.wait()
-    fast_out.wait()
 
 
 def solution(mesh):
@@ -491,11 +525,11 @@
         return pl.pallas_call(
             functools.partial(kernel, ny, nz, rs_lanes, ag_lanes),
             out_shape=(
-                jax.ShapeDtypeStruct((tok, feat), BF16),
-                jax.ShapeDtypeStruct((tok, feat), BF16),
+                pltpu.VMEM((tok, feat), BF16),
+                pltpu.VMEM((tok, feat), BF16),
             ),
             in_specs=[hbm] * 10,
-            out_specs=(hbm, hbm),
+            out_specs=(pl.BlockSpec(memory_space=vmem),) * 2,
             scratch_shapes=[
                 vmem((tok, feat), BF16),
                 vmem((2, tok, feat), BF16),
@@ -522,11 +556,8 @@
                 vmem((heads, tok, 1), F32),
                 vmem((heads, tok, 1), F32),
                 vmem((heads, tok, HEAD_DIM), F32),
-                vmem((tok, feat), BF16),
-                vmem((tok, feat), BF16),
                 dma((10,)),
-                dma((2,)),
-                dma((HOPS, 2)),
+                dma((HOPS + 1, 2)),
                 dma((HOPS, 2)),
                 dma((2,)),
                 dma((2,)),

time: 83.9 us -> 79.1 us (0.943)
  the two profiles are of different devices: /device:TPU:70 before, /device:TPU:1 now
where the time goes in v5:
time: 79.1 us; the launch traced here: 78.5 us
  Pallas kernels  76.4 us (97%)
  local copies, waits for them, and re-layouts  1.45 us (2%)
    pallas_call x1, Pallas kernels, body(): pl.pallas_call(functools.partial(kernel, ny, nz, rs_lanes, ag_lanes), out...  76.4 us

profile of v5, /device:TPU:1, one launch (start us, length us, event | category | flops | bytes accessed | tf_op | source)
XLA Modules:
  0.0 78.5 jit_solution(17107639196152071988)
XLA Ops:
  0.6 76.4 %shard_map.113 = (bf16[256,640]{1,0:T(8,128)(2,1)S(1)}, bf16[256,640]{1,0:T(8,128)(2,1)S(1)}) custom-call(bf16[256,640]{1,0:T(8,128)(2,1)} %aq_h.1, bf16[256,640]{1,0:T(8,128)(2,1)} %ak_h.1, bf16[256,640]{1,0:T(8,128)(2,1)} %av_h.1, bf16[256,640]{1,0:T(8,128)(2,1)} %fq_h.1, bf16[256,640]{1,0:T(8,128)(2,1)} %fk_h.1, bf16[256,640]{1,0:T(8,128)(2,1)} %fv_h.1, ...), custom_call_target="tpu_custom_call" | custom-call | tf_op jit(solution)/shard_map/pallas_call | solution.py:525
  77.1 0.7 copy.14
  77.8 0.7 copy.15

commit v6 on v5

--- a/solution.py
+++ b/solution.py
@@ -145,9 +145,6 @@
 
     scale = HEAD_DIM ** (-0.5) * LOG2_E
 
-    def alone(fn):
-        pl.when(s >= 0)(fn)
-
     def attend(delta, lo, hi):
         def one_head(h):
             cols = slice(h * HEAD_DIM, (h + 1) * HEAD_DIM)
@@ -175,10 +172,8 @@
                 acc_s[h] = acc_s[h] * alpha + jnp.dot(p.astype(BF16), val, preferred_element_type=F32)
 
         if delta == 0:
-            @alone
-            def _():
-                for h in range(lo, hi):
-                    one_head(h)
+            for h in range(lo, hi):
+                one_head(h)
         else:
             @pl.when(s >= delta)
             def _():
@@ -244,21 +239,15 @@
     def mate_terms(lo, hi):
         return rt[:, lo:hi]
 
-    @alone
-    def _():
-        add_grads(own_terms, 0, lanes_z, g_z, True)
-        add_grads(own_terms, 0, lanes_y, grad, True)
-
+    add_grads(own_terms, 0, lanes_z, g_z, True)
+    add_grads(own_terms, 0, lanes_y, grad, True)
     for i in range(6, 9):
         loads[i].wait()
     attend(0, 0, 1)
     term_copy.wait_recv()
     for part in range(2):
         pair_copy(part).wait_recv()
-    @alone
-    def _():
-        add_grads(mate_terms, 1, lanes_z, g_z, False)
-
+    add_grads(mate_terms, 1, lanes_z, g_z, False)
 
     def z_rows(i):
         return pl.ds(pl.multiple_of(lax.rem(z + i, nz) * zrow, zrow), zrow)
@@ -275,10 +264,7 @@
 
     for i in range(1, nz):
         zz_copy(i).start()
-    @alone
-    def _():
-        add_grads(mate_terms, 1, lanes_y, grad, False)
-
+    add_grads(mate_terms, 1, lanes_y, grad, False)
 
     def turn_z():
         got = g_z[:, z_rows(0), :]

time: 79.1 us -> 78.4 us (level)
  the two profiles are of different devices: /device:TPU:1 before, /device:TPU:458 now
where the time goes in v6:
time: 78.4 us; the launch traced here: 78.3 us
  Pallas kernels  76.2 us (97%)
  local copies, waits for them, and re-layouts  1.45 us (2%)
    pallas_call x1, Pallas kernels, body(): pl.pallas_call(functools.partial(kernel, ny, nz, rs_lanes, ag_lanes), out...  76.2 us

profile of v6, /device:TPU:458, one launch (start us, length us, event | category | flops | bytes accessed | tf_op | source)
XLA Modules:
  0.0 78.3 jit_solution(15711354656272577370)
XLA Ops:
  0.6 76.2 %shard_map.113 = (bf16[256,640]{1,0:T(8,128)(2,1)S(1)}, bf16[256,640]{1,0:T(8,128)(2,1)S(1)}) custom-call(bf16[256,640]{1,0:T(8,128)(2,1)} %aq_h.1, bf16[256,640]{1,0:T(8,128)(2,1)} %ak_h.1, bf16[256,640]{1,0:T(8,128)(2,1)} %av_h.1, bf16[256,640]{1,0:T(8,128)(2,1)} %fq_h.1, bf16[256,640]{1,0:T(8,128)(2,1)} %fk_h.1, bf16[256,640]{1,0:T(8,128)(2,1)} %fv_h.1, ...), custom_call_target="tpu_custom_call" | custom-call | tf_op jit(solution)/shard_map/pallas_call | solution.py:511
  76.8 0.7 copy.14
  77.5 0.7 copy.15
